TPU v7x, 32 devices: a whole 2x2x4 slice. The times are simulated.
32 devices in a mesh: ta: 4 (over y, core), xyz: 8 (over z, x).
Axes of the slice: x: 2, y: 2, z: 4, core: 2. Of those that a mesh axis runs over, the one named last changes fastest.
Arguments:
- prop_one: bfloat16 [4, 2, 12, 12, 32768], P('ta', None, None, None, 'xyz'), may hold values from -1.796875 to 1.796875
- prop_two: bfloat16 [4, 2, 12, 12, 32768], P('ta', None, None, None, 'xyz'), may hold values from -1.796875 to 1.796875
Outputs:
- momentum_fields: float32 [4, 16, 2, 32768], P(None, 'ta', None, 'xyz')
All inputs are finite; a program needn't handle non-finite values.
Results may differ from a plain program's by a relative error of at most 0.0003.
Values sent between devices are 32-bit elements; how exact they have to be, the bound alone decides.
A program may use at most 128 MiB of HBM per device.

v0:
```python
import functools
import math

import jax
import jax.numpy as jnp
import numpy as np
from jax import lax
from jax.experimental import pallas as pl
from jax.experimental.pallas import tpu as pltpu
from jax.sharding import PartitionSpec as P

L = 32


spin_columns = [[3, 2, 1, 0], [3, 2, 1, 0], [2, 3, 0, 1], [2, 3, 0, 1]]
spin_phases = [[1j, 1j, -1j, -1j], [-1.0, 1.0, 1.0, -1.0], [1j, -1j, -1j, 1j], [1.0, 1.0, 1.0, 1.0]]
chiral_signs = [1.0, 1.0, -1.0, -1.0]


def vertex_parts():
    result = []
    for gamma_index in range(4):
        columns = spin_columns[gamma_index]
        phases = spin_phases[gamma_index]
        rows_list = [columns[a // 3] * 3 + a % 3 for a in range(12)]
        phase_list = [complex(phases[a // 3]) for a in range(12)]
        result.append((rows_list, phase_list))
    return (result, [chiral_signs[a // 3] for a in range(12)])


def contract(prop_a, prop_b):
    gammas, chirality = vertex_parts()
    left_real, left_imag, right_real, right_imag = ([], [], [], [])
    for rows_list, phase_list in gammas:
        pick_real = jnp.stack([prop_a[0, q] for q in rows_list])
        pick_imag = jnp.stack([prop_a[1, q] for q in rows_list])
        phase_real = jnp.asarray(np.array([p.real for p in phase_list]), jnp.bfloat16)[
            :, None, None
        ]
        phase_imag = jnp.asarray(np.array([p.imag for p in phase_list]), jnp.bfloat16)[
            :, None, None
        ]
        left_real.append(phase_real * pick_real - phase_imag * pick_imag)
        left_imag.append(phase_real * pick_imag + phase_imag * pick_real)
        col_real = jnp.stack([prop_b[0][:, q] for q in rows_list], axis=1)
        col_imag = jnp.stack([prop_b[1][:, q] for q in rows_list], axis=1)
        factor = np.array(
            [
                [phase_list[c] * chirality[rows_list[c]] * chirality[a] for c in range(12)]
                for a in range(12)
            ]
        )
        factor_real = jnp.asarray(factor.real, jnp.bfloat16)[:, :, None]
        factor_imag = jnp.asarray(factor.imag, jnp.bfloat16)[:, :, None]
        right_real.append(factor_real * col_real + factor_imag * col_imag)
        right_imag.append(factor_imag * col_real - factor_real * col_imag)
    left_rows = jnp.stack(left_real + left_imag).reshape(8, 144, -1)
    right_rows = jnp.stack(right_real + right_imag).reshape(8, 144, -1)
    products = jnp.einsum("mks,nks->mns", left_rows, right_rows, preferred_element_type=jnp.float32)
    real_sum = products[:4, :4] - products[4:, 4:]
    imag_sum = products[:4, 4:] + products[4:, :4]
    return jnp.stack([real_sum.reshape(16, -1), imag_sum.reshape(16, -1)], axis=1)


def dft_tables(length):
    positions = np.arange(length)
    turn_count = positions[:, None] * positions[None, :] % length
    angles = turn_count * (2.0 * math.pi / length)
    cosines = jnp.asarray(np.cos(angles) / math.sqrt(length), jnp.float32)
    sines = jnp.asarray(np.sin(angles) / math.sqrt(length), jnp.float32)
    return (cosines, sines)


def plane_dft(fields):
    cosines, sines = dft_tables(L)
    highest = lax.Precision.HIGHEST
    shape = fields.shape
    grid = fields.reshape(shape[:4] + (L, L))
    real_part = grid[:, :, 0]
    imag_part = grid[:, :, 1]

    def along_z(values, table):
        return jnp.einsum(
            "tfpyz,zk->tfpyk", values, table, precision=highest, preferred_element_type=jnp.float32
        )

    def along_y(values, table):
        return jnp.einsum(
            "tfpyz,yk->tfpkz", values, table, precision=highest, preferred_element_type=jnp.float32
        )

    mid_real = along_z(real_part, cosines) + along_z(imag_part, sines)
    mid_imag = along_z(imag_part, cosines) - along_z(real_part, sines)
    out_real = along_y(mid_real, cosines) + along_y(mid_imag, sines)
    out_imag = along_y(mid_imag, cosines) - along_y(mid_real, sines)
    return jnp.stack([out_real, out_imag], axis=2).reshape(shape)


def line_dft(data):
    length = data.shape[-2]
    cosines, sines = dft_tables(length)
    real_part = data[..., 0, :, :]
    imag_part = data[..., 1, :, :]

    def transform_rows(values, table):
        return jnp.einsum(
            "...xq,xk->...qk",
            values,
            table,
            precision=lax.Precision.HIGHEST,
            preferred_element_type=jnp.float32,
        )

    out_real = transform_rows(real_part, cosines) + transform_rows(imag_part, sines)
    out_imag = transform_rows(imag_part, cosines) - transform_rows(real_part, sines)
    stacked = jnp.stack([out_real, out_imag], axis=-3)
    return stacked.reshape(stacked.shape[:-2] + (stacked.shape[-2] * stacked.shape[-1],))


def on_device(prop_one, prop_two):
    fields = lax.map(
        lambda slice_pair: contract(slice_pair[0], slice_pair[1]), (prop_one, prop_two)
    )
    local_times, field_count, parts, slab = fields.shape
    planes = slab // (L * L)
    fields = plane_dft(fields.reshape(local_times, field_count, parts, planes, L * L))
    turned_fields = line_dft(lax.all_to_all(fields, "xyz", split_axis=4, concat_axis=3, tiled=True))
    result = lax.all_to_all(turned_fields, "ta", split_axis=1, concat_axis=0, tiled=True)
    return result

LANES = 128
GROUP_PERMS = (0, 2)


def spin_tables():
    chi = np.array(chiral_signs)
    alpha = np.array(spin_phases) * chi[None, :]
    beta = np.array([[spin_phases[n][c] * chi[spin_columns[n][c]] for c in range(4)] for n in range(4)])
    tables = []
    for phases in (alpha, beta):
        pairs = []
        for first in GROUP_PERMS:
            found = []
            for a in range(4):
                for members in found:
                    ratio = phases[first : first + 2, a] / phases[first : first + 2, members[0][0]]
                    if ratio[0] == ratio[1] and ratio[0] in (1, -1):
                        members.append((a, int(ratio[0].real)))
                        break
                else:
                    found.append([(a, 1)])
            assert len(found) == 2
            pairs.append(found)
        lead = np.array([[phases[m, pairs[m // 2][half][0][0]] for half in range(2)] for m in range(4)])
        signs = np.array([[int((lead[m, half] / lead[m, 0]).real) for half in range(2)] for m in range(4)])
        tables.append((pairs, lead[:, 0], signs))
    left, right = tables
    phase = np.outer(left[1], right[1]).reshape(16)
    return left[0], left[2], right[0], right[2], phase


def complex_block(table):
    return np.block([[table.real, table.imag], [-table.imag, table.real]])


def high_low(table):
    high = np.asarray(table).astype(jnp.bfloat16)
    low = (table - high.astype(np.float64)).astype(jnp.bfloat16)
    return jnp.asarray(np.stack([high, low]))


def plane_tables(length):
    quarter = LANES // length
    outer = length // quarter
    lane = np.arange(LANES)
    y, z = lane // length, lane % length
    twiddle = np.exp(-2j * np.pi * np.outer(np.arange(outer), y) / length)
    ky, slot = lane // length, lane % length
    kz = (slot % outer) * quarter + slot // outer
    table = np.exp(-2j * np.pi * (np.outer(y, ky) / quarter + np.outer(z, kz) / length)) / length
    return (
        jnp.asarray(np.stack([twiddle.real, twiddle.imag]), jnp.float32),
        high_low(complex_block(table)),
    )


def line_table(length, own, sources):
    x = np.arange(length)
    turn = np.exp(-2j * np.pi * np.outer(x, x) / length) / math.sqrt(length)
    parts = complex_block(turn).reshape(2, sources, length // sources, 2, length)
    full = np.einsum("asxbk,fg->sxafbgk", parts, np.eye(own))
    rows = length * 2 * own
    return high_low(full.reshape(rows, rows))


def split_dot(values, table):
    high = values.astype(jnp.bfloat16)
    low = (values - high.astype(jnp.float32)).astype(jnp.bfloat16)

    def dot(a, b):
        return jnp.dot(a, b, preferred_element_type=jnp.float32)

    return dot(high, table[0]) + (dot(low, table[0]) + dot(high, table[1]))


def small_fft(values):
    count = len(values)
    if count == 1:
        return values
    even, odd = small_fft(values[0::2]), small_fft(values[1::2])
    low, high = [], []
    for k in range(count // 2):
        re, im = odd[k]
        if k == 0:
            pass
        elif 4 * k == count:
            re, im = im, -re
        else:
            c, s = math.cos(2 * math.pi * k / count), math.sin(2 * math.pi * k / count)
            re, im = c * re + s * im, c * im - s * re
        low.append((even[k][0] + re, even[k][1] + im))
        high.append((even[k][0] - re, even[k][1] - im))
    return low + high


def swap_blocks(values):
    width = LANES // 4
    shape = values[0].shape
    block = lax.broadcasted_iota(jnp.int32, shape, len(shape) - 1) // width
    axis = len(shape) - 1
    values = list(values)
    for step in (2, 1):
        keep = (block // step) % 2 == 0
        result = [None] * 4
        for i in range(4):
            if (i // step) % 2 == 0:
                a, b = values[i], values[i + step]
                result[i] = jnp.where(keep, a, pltpu.roll(b, step * width, axis))
                result[i + step] = jnp.where(keep, pltpu.roll(a, LANES - step * width, axis), b)
        values = result
    return values


def add_signed(total, term, sign):
    if total is None:
        return term if sign > 0 else -term
    return total + term if sign > 0 else total - term


def site_sums(tables, one_ref, two_ref, wide, turned, mixed):
    left_groups, left_signs, right_groups, right_signs, _ = tables
    rows = one_ref.shape[2]
    even = lax.broadcasted_iota(jnp.int32, (8, LANES), 0) % 2 == 0

    @pl.loop(0, 12)
    def _(a):
        for c in range(12):
            value = two_ref[a, c, :, :].astype(jnp.float32)
            wide[a, c, :, :] = value
            for at in range(0, rows, 8):
                piece = value[at : at + 8]
                turned[a, c, at : at + 8, :] = jnp.where(even, pltpu.roll(piece, 7, 0), pltpu.roll(piece, 1, 0))

    for pair in range(2):
        left_columns = spin_columns[GROUP_PERMS[pair]]
        sums = {}
        for half in range(2):
            for turn in range(2):
                right_columns = spin_columns[GROUP_PERMS[turn]]
                for side in range(2):
                    straight, crossed = None, None
                    for a, left_sign in left_groups[pair][half]:
                        for c, right_sign in right_groups[turn][side]:
                            for i in range(3):
                                for j in range(3):
                                    sink, source = left_columns[a] * 3 + i, c * 3 + j
                                    first = one_ref[sink, source, :, :].astype(jnp.float32)
                                    at = (a * 3 + i, right_columns[c] * 3 + j)
                                    sign = left_sign * right_sign
                                    straight = add_signed(straight, first * wide[at[0], at[1], :, :], sign)
                                    crossed = add_signed(crossed, first * turned[at[0], at[1], :, :], sign)
                    sums[half, turn, side] = (straight, crossed)
        for mu in (2 * pair, 2 * pair + 1):
            for nu in range(4):
                for kind in range(2):
                    total = None
                    for half in range(2):
                        for side in range(2):
                            sign = int(left_signs[mu][half] * right_signs[nu][side])
                            total = add_signed(total, sums[half, nu // 2, side][kind], sign)
                    start = (4 * mu + nu) * rows
                    mixed[kind, start : start + rows, :] = total


def plane_blocks(phase_ref, twiddle_ref, plane_ref, mixed, tiles, store):
    blocks = []
    for t in range(tiles):
        straight = [mixed[0, pl.ds(2 * t + part, 16, stride=2 * tiles), :] for part in range(2)]
        crossed = [mixed[1, pl.ds(2 * t + part, 16, stride=2 * tiles), :] for part in range(2)]
        re, im = straight[0] + straight[1], crossed[1] - crossed[0]
        c, s = phase_ref[0], phase_ref[1]
        blocks.append((c * re - s * im, c * im + s * re))
    spectrum = small_fft(blocks)
    turned = []
    for k, (re, im) in enumerate(spectrum):
        c = twiddle_ref[0, k : k + 1, :]
        s = twiddle_ref[1, k : k + 1, :]
        turned.append(jnp.concatenate([re * c - im * s, re * s + im * c], axis=1) if k else jnp.concatenate([re, im], axis=1))
    out = split_dot(jnp.concatenate(turned, axis=0), plane_ref)
    upper = lax.broadcasted_iota(jnp.int32, (8, LANES), 0) < 4
    for half in range(tiles // 4):
        parts = []
        for part in range(2):
            rows = [
                out[(4 * half + p) * 16 : (4 * half + p + 1) * 16, part * LANES : (part + 1) * LANES]
                for p in range(4)
            ]
            parts.append(swap_blocks(rows))
        for k in range(4):
            owner = k * (tiles // 4) + half
            for pair in range(2):
                re = parts[0][k][pair * 8 : pair * 8 + 8]
                im = parts[1][k][pair * 8 : pair * 8 + 8]
                store(owner, 2 * pair, jnp.where(upper, re, pltpu.roll(im, 4, 0)))
                store(owner, 2 * pair + 1, jnp.where(upper, pltpu.roll(re, 4, 0), im))


def finish_time(rows, line_ref, out_ref, at, own):
    out = split_dot(rows.T, line_ref)
    for part in range(2):
        grid = out[:, part * LANES : (part + 1) * LANES].reshape(4, 4, 8, LANES)
        done = swap_blocks([grid[:, q].reshape(32, LANES) for q in range(4)])
        for f in range(own):
            out_ref[at, f, pl.ds(part, 32, stride=2), :] = done[f]


def fused_kernel(
    tables, tiles, planes, times, sources, own, names,
    one_ref, two_ref, phase_ref, twiddle_ref, plane_ref, line_ref, out_ref,
    wide, turned, mixed, send, got, send_sem, recv_sem,
):
    step = pl.program_id(0)
    t, s = lax.axis_index(names[0]), lax.axis_index(names[1])
    far = sorted(range(sources), key=lambda o: -min(o, sources - o))
    offsets = [(a, o) for o in far for a in reversed(range(times)) if (a, o) != (0, 0)]
    barrier = pltpu.get_barrier_semaphore()

    def peer(a, o):
        return lax.rem(t + a, times), lax.rem(s + o, sources)

    def copy(x, k):
        to_t, to_s = peer(*offsets[k])
        return pltpu.make_async_remote_copy(
            src_ref=send.at[to_s, to_t, x],
            dst_ref=got.at[t, s, x],
            send_sem=send_sem.at[x, k],
            recv_sem=recv_sem.at[x, k],
            device_id={names[0]: to_t, names[1]: to_s},
            device_id_type=pl.DeviceIdType.MESH,
        )

    def arrival(x, k):
        a, o = offsets[k]
        from_t, from_s = peer(times - a, sources - o)
        return pltpu.make_async_remote_copy(
            src_ref=send.at[from_s, from_t, x],
            dst_ref=got.at[from_t, from_s, x],
            send_sem=send_sem.at[x, k],
            recv_sem=recv_sem.at[x, k],
            device_id={names[0]: from_t, names[1]: from_s},
            device_id_type=pl.DeviceIdType.MESH,
        )

    @pl.when(step == 0)
    def _():
        for a, o in offsets:
            to_t, to_s = peer(a, o)
            pl.semaphore_signal(
                barrier, inc=1, device_id={names[0]: to_t, names[1]: to_s}, device_id_type=pl.DeviceIdType.MESH
            )

    site_sums(tables, one_ref, two_ref, wide, turned, mixed)

    def store(owner, group, value):
        send[owner, group, step, :, :] = value

    plane_blocks(phase_ref, twiddle_ref, plane_ref, mixed, tiles, store)

    @pl.when(step == 0)
    def _():
        pl.semaphore_wait(barrier, len(offsets))

    for k in range(len(offsets)):
        copy(step, k).start()
    got[t, s, step, :, :] = send[s, t, step, :, :]

    @pl.when(step == planes - 1)
    def _():
        for a in range(times):
            @pl.loop(0, planes)
            def _(x):
                for k in range(len(offsets)):
                    if offsets[k][0] == a:
                        arrival(x, k).wait_recv()
                        copy(x, k).wait_send()
            from_t = lax.rem(t + times - a, times)
            rows = got[from_t].reshape(sources * planes * 8, LANES)
            finish_time(rows, line_ref, out_ref, from_t, own)


def fast_device(prop_one, prop_two, times, sources):
    slab = prop_one.shape[-1]
    plane = L * L
    planes, tiles = slab // plane, plane // LANES
    own = 16 // times
    tables = spin_tables()
    twiddle, plane_table = plane_tables(L)
    line = line_table(L, own, sources)
    phase = np.broadcast_to(tables[4][:, None], (16, LANES))
    phase = jnp.asarray(np.stack([phase.real, phase.imag]), jnp.float32)

    def paired(prop):
        split = prop.reshape(2, 12, 12, slab // LANES, LANES).transpose(1, 2, 3, 0, 4)
        return split.reshape(12, 12, slab // LANES * 2, LANES)

    block = pl.BlockSpec((12, 12, 2 * tiles, LANES), lambda x: (0, 0, x, 0))

    def whole(shape):
        return pl.BlockSpec(shape, lambda x: (0,) * len(shape))

    peers = times * sources - 1
    shape = (times, own, slab * 2 // LANES, LANES)
    out = pl.pallas_call(
        functools.partial(fused_kernel, tables, tiles, planes, times, sources, own, ("ta", "xyz")),
        grid=(planes,),
        out_shape=jax.ShapeDtypeStruct(shape, jnp.float32),
        in_specs=[block, block] + [whole(v.shape) for v in (phase, twiddle, plane_table, line)],
        out_specs=whole(shape),
        scratch_shapes=[
            pltpu.VMEM((12, 12, 2 * tiles, LANES), jnp.float32),
            pltpu.VMEM((12, 12, 2 * tiles, LANES), jnp.float32),
            pltpu.VMEM((2, 16 * 2 * tiles, LANES), jnp.float32),
            pltpu.VMEM((sources, times, planes, 8, LANES), jnp.float32),
            pltpu.VMEM((times, sources, planes, 8, LANES), jnp.float32),
            pltpu.SemaphoreType.DMA((planes, peers)),
            pltpu.SemaphoreType.DMA((planes, peers)),
        ],
        compiler_params=pltpu.CompilerParams(
            collective_id=0, has_side_effects=True, dimension_semantics=("arbitrary",)
        ),
    )(paired(prop_one), paired(prop_two), phase, twiddle, plane_table, line)
    return out.reshape(times, own, slab // LANES, 2, LANES).transpose(0, 1, 3, 2, 4).reshape(times, own, 2, slab)


def solution(mesh):
    placed = (P("ta", None, None, None, "xyz"), P("ta", None, None, None, "xyz"))
    times, sources = mesh.shape["ta"], mesh.shape["xyz"]

    def device(prop_one, prop_two):
        planes = prop_one.shape[-1] // (L * L)
        fits = 4 * L == LANES and planes * sources == L and L // sources == 4 and times == 4
        if fits and prop_one.shape[0] == 1:
            return fast_device(prop_one, prop_two, times, sources)
        return on_device(prop_one, prop_two)

    return jax.shard_map(
        device, mesh=mesh, in_specs=placed, out_specs=P(None, "ta", None, "xyz"), check_vma=False
    )
```

profile of v0, /device:TPU:0, one launch (start us, length us, event | category | flops | bytes accessed | tf_op | source)
XLA Modules:
  0.0 27.7 jit_solution(16564744312796976526)
XLA Ops:
  0.0 25.8 %shard_map.64 = f32[4,4,64,128]{3,2,1,0:T(8,128)} custom-call(bf16[12,12,64,128]{3,2,1,0:T(8,128)(2,1)} %bitcast.15, bf16[12,12,64,128]{3,2,1,0:T(8,128)(2,1)} %bitcast.16, f32[2,16,128]{2,1,0:T(8,128)} %constant.11.clone.phase_ref, f32[2,8,128]{2,1,0:T(8,128)} %constant.8.clone.twiddle_ref, bf16[2,256,256]{2,1,0:T(8,128)(2,1)} %constant.9.clone.plane_ref, ...), custom_call_target="tpu_custom_call" | custom-call | tf_op jit(solution)/shard_map/pallas_call | solution.py:433
  25.8 1.9 %copy.11 = f32[4,4,2,4096]{3,2,1,0:T(2,128)} copy(f32[4,4,2,4096]{3,2,1,0:T(2,128)} %bitcast.17) | data formatting | bytes 1048576
where the time goes:
time: 27.9 us; the launch traced here: 27.7 us
  Pallas kernels  25.8 us (92%)
  local copies, waits for them, and re-layouts  1.89 us (7%)
    pallas_call x1, Pallas kernels, fast_device(): pl.pallas_call(functools.partial(fused_kernel, tables, tiles, planes, tim...  25.8 us
    unnamed x1, local copies, waits for them, and re-layouts  1.89 us

commit v1 on v0

--- a/solution.py
+++ b/solution.py
@@ -247,15 +247,16 @@
     return total + term if sign > 0 else total - term
 
 
-def site_sums(tables, one_ref, two_ref, wide, turned, mixed):
+def site_sums(tables, one_ref, two_ref, wide, turned, mixed, row):
     left_groups, left_signs, right_groups, right_signs, _ = tables
-    rows = one_ref.shape[2]
+    rows = wide.shape[2]
     even = lax.broadcasted_iota(jnp.int32, (8, LANES), 0) % 2 == 0
+    span = pl.ds(row, rows)
 
     @pl.loop(0, 12)
     def _(a):
         for c in range(12):
-            value = two_ref[a, c, :, :].astype(jnp.float32)
+            value = two_ref[a, c, span, :].astype(jnp.float32)
             wide[a, c, :, :] = value
             for at in range(0, rows, 8):
                 piece = value[at : at + 8]
@@ -274,7 +275,7 @@
                             for i in range(3):
                                 for j in range(3):
                                     sink, source = left_columns[a] * 3 + i, c * 3 + j
-                                    first = one_ref[sink, source, :, :].astype(jnp.float32)
+                                    first = one_ref[sink, source, span, :].astype(jnp.float32)
                                     at = (a * 3 + i, right_columns[c] * 3 + j)
                                     sign = left_sign * right_sign
                                     straight = add_signed(straight, first * wide[at[0], at[1], :, :], sign)
@@ -334,78 +335,115 @@
             out_ref[at, f, pl.ds(part, 32, stride=2), :] = done[f]
 
 
-def fused_kernel(
-    tables, tiles, planes, times, sources, own, names,
-    one_ref, two_ref, phase_ref, twiddle_ref, plane_ref, line_ref, out_ref,
-    wide, turned, mixed, send, got, send_sem, recv_sem,
+def peers_of(t, s, times, sources):
+    y, core, z, x = t // 2, t % 2, s // 2, s % 2
+    own_half, other_half = z // 2 * 2, (1 - z // 2) * 2
+    near, far = (z + 1) % 2, z % 2
+    levels = [other_half, other_half + 1, own_half + near, own_half + far]
+    result = []
+    for level in range(4):
+        for plane in range(8):
+            dy, dx, dc = plane // 4, plane // 2 % 2, plane % 2
+            if level == 3 and plane == 0:
+                continue
+            result.append(((y + dy) % 2 * 2 + (core + dc) % 2, levels[level] * 2 + (x + dx) % 2))
+    return result
+
+
+def exchange_kernel(
+    tables, tiles, planes, times, sources, names,
+    one_hbm, two_hbm, phase_hbm, twiddle_hbm, plane_hbm, line_hbm, got, line_out,
+    one_ref, two_ref, phase_ref, twiddle_ref, plane_ref, wide, turned, mixed, send,
+    in_sem, table_sem, send_sem, recv_sem,
 ):
-    step = pl.program_id(0)
     t, s = lax.axis_index(names[0]), lax.axis_index(names[1])
-    far = sorted(range(sources), key=lambda o: -min(o, sources - o))
-    offsets = [(a, o) for o in far for a in reversed(range(times)) if (a, o) != (0, 0)]
     barrier = pltpu.get_barrier_semaphore()
-
-    def peer(a, o):
-        return lax.rem(t + a, times), lax.rem(s + o, sources)
-
-    def copy(x, k):
-        to_t, to_s = peer(*offsets[k])
-        return pltpu.make_async_remote_copy(
-            src_ref=send.at[to_s, to_t, x],
-            dst_ref=got.at[t, s, x],
-            send_sem=send_sem.at[x, k],
-            recv_sem=recv_sem.at[x, k],
-            device_id={names[0]: to_t, names[1]: to_s},
-            device_id_type=pl.DeviceIdType.MESH,
+    peers = peers_of(t, s, times, sources)
+    count = len(peers)
+
+    def device(k):
+        return {names[0]: peers[k][0], names[1]: peers[k][1]}
+
+    def load(p, which):
+        source, target = ((one_hbm, one_ref), (two_hbm, two_ref))[which]
+        rows = pl.ds(pl.multiple_of(p * 2 * tiles, 2 * tiles), 2 * tiles)
+        return pltpu.make_async_copy(source.at[:, :, rows, :], target.at[:, :, rows, :], in_sem.at[which, p])
+
+    table_copies = [
+        pltpu.make_async_copy(source, target, table_sem.at[k])
+        for k, (source, target) in enumerate(
+            ((phase_hbm, phase_ref), (twiddle_hbm, twiddle_ref), (plane_hbm, plane_ref), (line_hbm, line_out))
         )
-
-    def arrival(x, k):
-        a, o = offsets[k]
-        from_t, from_s = peer(times - a, sources - o)
-        return pltpu.make_async_remote_copy(
-            src_ref=send.at[from_s, from_t, x],
-            dst_ref=got.at[from_t, from_s, x],
-            send_sem=send_sem.at[x, k],
-            recv_sem=recv_sem.at[x, k],
-            device_id={names[0]: from_t, names[1]: from_s},
-            device_id_type=pl.DeviceIdType.MESH,
-        )
-
-    @pl.when(step == 0)
-    def _():
-        for a, o in offsets:
-            to_t, to_s = peer(a, o)
-            pl.semaphore_signal(
-                barrier, inc=1, device_id={names[0]: to_t, names[1]: to_s}, device_id_type=pl.DeviceIdType.MESH
-            )
-
-    site_sums(tables, one_ref, two_ref, wide, turned, mixed)
-
-    def store(owner, group, value):
-        send[owner, group, step, :, :] = value
-
-    plane_blocks(phase_ref, twiddle_ref, plane_ref, mixed, tiles, store)
-
-    @pl.when(step == 0)
-    def _():
-        pl.semaphore_wait(barrier, len(offsets))
-
-    for k in range(len(offsets)):
-        copy(step, k).start()
-    got[t, s, step, :, :] = send[s, t, step, :, :]
-
-    @pl.when(step == planes - 1)
-    def _():
-        for a in range(times):
-            @pl.loop(0, planes)
-            def _(x):
-                for k in range(len(offsets)):
-                    if offsets[k][0] == a:
-                        arrival(x, k).wait_recv()
-                        copy(x, k).wait_send()
-            from_t = lax.rem(t + times - a, times)
-            rows = got[from_t].reshape(sources * planes * 8, LANES)
-            finish_time(rows, line_ref, out_ref, from_t, own)
+    ]
+    for which in (1, 0):
+        load(0, which).start()
+    for k in range(count):
+        pl.semaphore_signal(barrier, inc=1, device_id=device(k), device_id_type=pl.DeviceIdType.MESH)
+    for copy in table_copies[:3]:
+        copy.start()
+    for p in range(1, planes):
+        for which in (1, 0):
+            load(p, which).start()
+    table_copies[3].start()
+
+    @pl.loop(0, planes)
+    def _(p):
+        load(p, 1).wait()
+        load(p, 0).wait()
+        row = pl.multiple_of(p * 2 * tiles, 2 * tiles)
+        site_sums(tables, one_ref, two_ref, wide, turned, mixed, row)
+
+        @pl.when(p == 0)
+        def _():
+            for copy in table_copies[:3]:
+                copy.wait()
+
+        def store(owner, group, value):
+            send[group * sources + owner, p, :, :] = value
+
+        plane_blocks(phase_ref, twiddle_ref, plane_ref, mixed, tiles, store)
+
+        @pl.when(p == 0)
+        def _():
+            pl.semaphore_wait(barrier, count)
+
+        for k in range(count):
+            to_t, to_s = peers[k]
+            pltpu.make_async_remote_copy(
+                src_ref=send.at[to_t * sources + to_s, p],
+                dst_ref=got.at[t * sources + s, p],
+                send_sem=send_sem,
+                recv_sem=recv_sem,
+                device_id=device(k),
+                device_id_type=pl.DeviceIdType.MESH,
+            ).start()
+        own = t * sources + s
+        got[own, p, :, :] = send[own, p, :, :]
+
+    table_copies[3].wait()
+    everything = pltpu.make_async_remote_copy(
+        src_ref=send.at[pl.ds(0, count)],
+        dst_ref=got.at[pl.ds(0, count)],
+        send_sem=send_sem,
+        recv_sem=recv_sem,
+        device_id=device(0),
+        device_id_type=pl.DeviceIdType.MESH,
+    )
+    everything.wait_recv()
+    everything.wait_send()
+
+
+def finish_kernel(times, own, got, line_ref, out_hbm, out_ref, out_sem):
+    copies = []
+    for at in range(times):
+        span = got.shape[0] // times
+        rows = got[at * span : (at + 1) * span].reshape(-1, LANES)
+        finish_time(rows, line_ref, out_ref, at, own)
+        copy = pltpu.make_async_copy(out_ref.at[at], out_hbm.at[at], out_sem.at[at])
+        copy.start()
+        copies.append(copy)
+    for copy in copies:
+        copy.wait()
 
 
 def fast_device(prop_one, prop_two, times, sources):
@@ -423,32 +461,46 @@
         split = prop.reshape(2, 12, 12, slab // LANES, LANES).transpose(1, 2, 3, 0, 4)
         return split.reshape(12, 12, slab // LANES * 2, LANES)
 
-    block = pl.BlockSpec((12, 12, 2 * tiles, LANES), lambda x: (0, 0, x, 0))
-
-    def whole(shape):
-        return pl.BlockSpec(shape, lambda x: (0,) * len(shape))
-
-    peers = times * sources - 1
-    shape = (times, own, slab * 2 // LANES, LANES)
-    out = pl.pallas_call(
-        functools.partial(fused_kernel, tables, tiles, planes, times, sources, own, ("ta", "xyz")),
-        grid=(planes,),
-        out_shape=jax.ShapeDtypeStruct(shape, jnp.float32),
-        in_specs=[block, block] + [whole(v.shape) for v in (phase, twiddle, plane_table, line)],
-        out_specs=whole(shape),
+    anywhere = pl.BlockSpec(memory_space=pltpu.HBM)
+    vmem = pl.BlockSpec(memory_space=pltpu.VMEM)
+    everyone = times * sources
+    inputs = (paired(prop_one), paired(prop_two), phase, twiddle, plane_table, line)
+    got, line_near = pl.pallas_call(
+        functools.partial(exchange_kernel, tables, tiles, planes, times, sources, ("ta", "xyz")),
+        out_shape=(
+            pltpu.VMEM((everyone, planes, 8, LANES), jnp.float32),
+            pltpu.VMEM(line.shape, line.dtype),
+        ),
+        in_specs=[anywhere] * len(inputs),
+        out_specs=(vmem, vmem),
         scratch_shapes=[
+            pltpu.VMEM((12, 12, slab // LANES * 2, LANES), jnp.bfloat16),
+            pltpu.VMEM((12, 12, slab // LANES * 2, LANES), jnp.bfloat16),
+            pltpu.VMEM(phase.shape, phase.dtype),
+            pltpu.VMEM(twiddle.shape, twiddle.dtype),
+            pltpu.VMEM(plane_table.shape, plane_table.dtype),
             pltpu.VMEM((12, 12, 2 * tiles, LANES), jnp.float32),
             pltpu.VMEM((12, 12, 2 * tiles, LANES), jnp.float32),
             pltpu.VMEM((2, 16 * 2 * tiles, LANES), jnp.float32),
-            pltpu.VMEM((sources, times, planes, 8, LANES), jnp.float32),
-            pltpu.VMEM((times, sources, planes, 8, LANES), jnp.float32),
-            pltpu.SemaphoreType.DMA((planes, peers)),
-            pltpu.SemaphoreType.DMA((planes, peers)),
+            pltpu.VMEM((everyone, planes, 8, LANES), jnp.float32),
+            pltpu.SemaphoreType.DMA((2, planes)),
+            pltpu.SemaphoreType.DMA((4,)),
+            pltpu.SemaphoreType.DMA,
+            pltpu.SemaphoreType.DMA,
         ],
         compiler_params=pltpu.CompilerParams(
-            collective_id=0, has_side_effects=True, dimension_semantics=("arbitrary",)
+            collective_id=0, has_side_effects=True, vmem_limit_bytes=40 * 2**20
         ),
-    )(paired(prop_one), paired(prop_two), phase, twiddle, plane_table, line)
+    )(*inputs)
+    shape = (times, own, slab * 2 // LANES, LANES)
+    out = pl.pallas_call(
+        functools.partial(finish_kernel, times, own),
+        out_shape=jax.ShapeDtypeStruct(shape, jnp.float32),
+        in_specs=[vmem, vmem],
+        out_specs=anywhere,
+        scratch_shapes=[pltpu.VMEM(shape, jnp.float32), pltpu.SemaphoreType.DMA((times,))],
+        compiler_params=pltpu.CompilerParams(vmem_limit_bytes=40 * 2**20),
+    )(got, line_near)
     return out.reshape(times, own, slab // LANES, 2, LANES).transpose(0, 1, 3, 2, 4).reshape(times, own, 2, slab)
 
 

time: 27.9 us -> 28.7 us (1.029)
  local copies, waits for them, and re-layouts: 1.89 us -> 6.64 us
  Pallas kernels: 25.8 us -> 21.7 us
    unnamed x1 -> x12, local copies, waits for them, and re-layouts: 1.89 us -> 6.64 us
    pallas_call x1 -> x2, Pallas kernels: 25.8 us -> 21.7 us  [the longest x1 20.3 us: fast_device(): pl.pallas_call(functools.partial(exchange_kernel, tables, tiles, planes,...]
where the time goes in v1:
time: 28.7 us; the launch traced here: 28.4 us
  Pallas kernels  21.7 us (76%)
  local copies, waits for them, and re-layouts  6.64 us (23%)
    pallas_call x1, Pallas kernels, fast_device(): pl.pallas_call(functools.partial(exchange_kernel, tables, tiles, planes,...  20.3 us
    unnamed x12, local copies, waits for them, and re-layouts  6.64 us
    pallas_call x1, Pallas kernels, fast_device(): pl.pallas_call(functools.partial(finish_kernel, times, own), out_shape=ja...  1.42 us

profile of v1, /device:TPU:0, one launch (start us, length us, event | category | flops | bytes accessed | tf_op | source)
XLA Modules:
  0.0 28.4 jit_solution(13978400067527443943)
XLA Ops:
  0.0 0.0 copy-start
  0.0 1.7 %copy-done = bf16[1,2,12,12,4096]{4,1,3,2,0:T(2,128)(2,1)S(1)} copy-done((bf16[1,2,12,12,4096]{4,1,3,2,0:T(2,128)(2,1)S(1)}, bf16[1,2,12,12,4096]{4,1,3,2,0:T(2,128)(2,1)}, u32[]{:S(2)}) %copy-start) | copy-done | bytes 2359320
  1.7 0.0 copy-start.1
  1.7 1.7 %copy-done.1 = bf16[1,2,12,12,4096]{4,1,3,2,0:T(2,128)(2,1)S(1)} copy-done((bf16[1,2,12,12,4096]{4,1,3,2,0:T(2,128)(2,1)S(1)}, bf16[1,2,12,12,4096]{4,1,3,2,0:T(2,128)(2,1)}, u32[]{:S(2)}) %copy-start.1) | copy-done | bytes 2359320
  3.3 0.0 copy-start.2
  3.3 0.9 %copy-done.2 = bf16[2,256,256]{2,1,0:T(8,128)(2,1)S(1)} copy-done((bf16[2,256,256]{2,1,0:T(8,128)(2,1)S(1)}, bf16[2,256,256]{2,1,0:T(8,128)(2,1)}, u32[]{:S(2)}) %copy-start.2) | copy-done | bytes 262168
  4.3 0.0 copy-start.3
  4.3 0.9 %copy-done.3 = bf16[2,256,256]{2,1,0:T(8,128)(2,1)S(1)} copy-done((bf16[2,256,256]{2,1,0:T(8,128)(2,1)S(1)}, bf16[2,256,256]{2,1,0:T(8,128)(2,1)}, u32[]{:S(2)}) %copy-start.3) | copy-done | bytes 262168
  5.2 0.0 copy-start.4
  5.2 0.7 %copy-done.4 = f32[2,16,128]{2,1,0:T(8,128)S(1)} copy-done((f32[2,16,128]{2,1,0:T(8,128)S(1)}, f32[2,16,128]{2,1,0:T(8,128)}, u32[]{:S(2)}) %copy-start.4) | copy-done | bytes 16408
  6.0 0.0 copy-start.5
  6.0 0.7 %copy-done.5 = f32[2,8,128]{2,1,0:T(8,128)S(1)} copy-done((f32[2,8,128]{2,1,0:T(8,128)S(1)}, f32[2,8,128]{2,1,0:T(8,128)}, u32[]{:S(2)}) %copy-start.5) | copy-done | bytes 8216
  6.6 20.3 %shard_map.64 = (f32[32,4,8,128]{3,2,1,0:T(8,128)S(1)}, bf16[2,256,256]{2,1,0:T(8,128)(2,1)S(1)}) custom-call(bf16[12,12,64,128]{3,2,1,0:T(8,128)(2,1)S(1)} %bitcast.15, bf16[12,12,64,128]{3,2,1,0:T(8,128)(2,1)S(1)} %bitcast.16, f32[2,16,128]{2,1,0:T(8,128)S(1)} %copy-done.4, f32[2,8,128]{2,1,0:T(8,128)S(1)} %copy-done.5, ...), custom_call_target="tpu_custom_call" | custom-call | tf_op jit(solution)/shard_map/pallas_call | solution.py:468
  27.0 1.4 %shard_map.65 = f32[4,4,64,128]{3,2,1,0:T(8,128)} custom-call(f32[32,4,8,128]{3,2,1,0:T(8,128)S(1)} %get-tuple-element.7.got, bf16[2,256,256]{2,1,0:T(8,128)(2,1)S(1)} %get-tuple-element.8.line_ref), custom_call_target="tpu_custom_call" | custom-call | tf_op jit(solution)/shard_map/pallas_call | solution.py:496
Async XLA Ops:
  0.0 1.7 %copy-start = (bf16[1,2,12,12,4096]{4,1,3,2,0:T(2,128)(2,1)S(1)}, bf16[1,2,12,12,4096]{4,1,3,2,0:T(2,128)(2,1)}, u32[]{:S(2)}) copy-start(bf16[1,2,12,12,4096]{4,1,3,2,0:T(2,128)(2,1)} %param.6) | copy-start | bytes 7077892
  1.7 1.7 %copy-start.1 = (bf16[1,2,12,12,4096]{4,1,3,2,0:T(2,128)(2,1)S(1)}, bf16[1,2,12,12,4096]{4,1,3,2,0:T(2,128)(2,1)}, u32[]{:S(2)}) copy-start(bf16[1,2,12,12,4096]{4,1,3,2,0:T(2,128)(2,1)} %param.7) | copy-start | bytes 7077892
  3.3 0.9 %copy-start.2 = (bf16[2,256,256]{2,1,0:T(8,128)(2,1)S(1)}, bf16[2,256,256]{2,1,0:T(8,128)(2,1)}, u32[]{:S(2)}) copy-start(bf16[2,256,256]{2,1,0:T(8,128)(2,1)} %constant.10.clone.line_hbm) | copy-start | bytes 786436
  4.3 0.9 %copy-start.3 = (bf16[2,256,256]{2,1,0:T(8,128)(2,1)S(1)}, bf16[2,256,256]{2,1,0:T(8,128)(2,1)}, u32[]{:S(2)}) copy-start(bf16[2,256,256]{2,1,0:T(8,128)(2,1)} %constant.9.clone.plane_hbm) | copy-start | bytes 786436
  5.2 0.7 %copy-start.4 = (f32[2,16,128]{2,1,0:T(8,128)S(1)}, f32[2,16,128]{2,1,0:T(8,128)}, u32[]{:S(2)}) copy-start(f32[2,16,128]{2,1,0:T(8,128)} %constant.11.clone.phase_hbm) | copy-start | bytes 49156
  6.0 0.7 %copy-start.5 = (f32[2,8,128]{2,1,0:T(8,128)S(1)}, f32[2,8,128]{2,1,0:T(8,128)}, u32[]{:S(2)}) copy-start(f32[2,8,128]{2,1,0:T(8,128)} %constant.8.clone.twiddle_hbm) | copy-start | bytes 24580

commit v2 on v1

--- a/solution.py
+++ b/solution.py
@@ -491,7 +491,7 @@
         compiler_params=pltpu.CompilerParams(
             collective_id=0, has_side_effects=True, vmem_limit_bytes=40 * 2**20
         ),
-    )(*inputs)
+    )(*[pltpu.with_memory_space_constraint(v, pltpu.HBM) for v in inputs])
     shape = (times, own, slab * 2 // LANES, LANES)
     out = pl.pallas_call(
         functools.partial(finish_kernel, times, own),

time: 28.7 us -> 22.2 us (0.77)
  local copies, waits for them, and re-layouts: 6.64 us -> 0 us
  Pallas kernels: 21.7 us -> 22.1 us
    unnamed x12 -> x0, local copies, waits for them, and re-layouts: 6.64 us -> none
    pallas_call x1, Pallas kernels: 20.3 us -> 20.7 us  [fast_device(): pl.pallas_call(functools.partial(exchange_kernel, tables, tiles, planes,...]
where the time goes in v2:
time: 22.2 us; the launch traced here: 22.1 us
  Pallas kernels  22.1 us (100%)
    pallas_call x1, Pallas kernels, fast_device(): pl.pallas_call(functools.partial(exchange_kernel, tables, tiles, planes,...  20.7 us
    pallas_call x1, Pallas kernels, fast_device(): pl.pallas_call(functools.partial(finish_kernel, times, own), out_shape=ja...  1.41 us

profile of v2, /device:TPU:0, one launch (start us, length us, event | category | flops | bytes accessed | tf_op | source)
XLA Modules:
  0.0 22.1 jit_solution(8857664954131905582)
XLA Ops:
  0.0 20.7 %shard_map.64 = (f32[32,4,8,128]{3,2,1,0:T(8,128)S(1)}, bf16[2,256,256]{2,1,0:T(8,128)(2,1)S(1)}) custom-call(bf16[12,12,64,128]{3,2,1,0:T(8,128)(2,1)} %bitcast.15, bf16[12,12,64,128]{3,2,1,0:T(8,128)(2,1)} %bitcast.16, f32[2,16,128]{2,1,0:T(8,128)} %constant.11.clone.phase_hbm, f32[2,8,128]{2,1,0:T(8,128)} %constant.8.clone.twiddle_hbm, ...), custom_call_target="tpu_custom_call" | custom-call | tf_op jit(solution)/shard_map/pallas_call | solution.py:468
  20.7 1.4 %shard_map.65 = f32[4,4,64,128]{3,2,1,0:T(8,128)} custom-call(f32[32,4,8,128]{3,2,1,0:T(8,128)S(1)} %get-tuple-element.7.got, bf16[2,256,256]{2,1,0:T(8,128)(2,1)S(1)} %get-tuple-element.8.line_ref), custom_call_target="tpu_custom_call" | custom-call | tf_op jit(solution)/shard_map/pallas_call | solution.py:496

commit v3 on v2

--- a/solution.py
+++ b/solution.py
@@ -335,18 +335,30 @@
             out_ref[at, f, pl.ds(part, 32, stride=2), :] = done[f]
 
 
-def peers_of(t, s, times, sources):
+def peers_of(t, s, late):
     y, core, z, x = t // 2, t % 2, s // 2, s % 2
     own_half, other_half = z // 2 * 2, (1 - z // 2) * 2
-    near, far = (z + 1) % 2, z % 2
-    levels = [other_half, other_half + 1, own_half + near, own_half + far]
+    edge = 3 * (1 - z // 2)
+    inner = edge + 2 * (z // 2) - 1
+    near, far = own_half + (z + 1) % 2, z
+    relative = []
+    for level in (edge, inner, near, far):
+        for plane in reversed(range(8)):
+            dy, dx, dc = plane // 4, plane // 2 % 2, plane % 2
+            if level is far and plane == 0:
+                continue
+            relative.append(((y + dy) % 2 * 2 + (core + dc) % 2, level * 2 + (x + dx) % 2))
+    if not late:
+        return relative
+    first, second = (edge, inner)
     result = []
-    for level in range(4):
+    for level in (edge, inner, near):
         for plane in range(8):
             dy, dx, dc = plane // 4, plane // 2 % 2, plane % 2
-            if level == 3 and plane == 0:
-                continue
-            result.append(((y + dy) % 2 * 2 + (core + dc) % 2, levels[level] * 2 + (x + dx) % 2))
+            result.append((dy * 2 + (core + dc) % 2, level * 2 + dx))
+    for plane in reversed(range(1, 8)):
+        dy, dx, dc = plane // 4, plane // 2 % 2, plane % 2
+        result.append(((y + dy) % 2 * 2 + (core + dc) % 2, far * 2 + (x + dx) % 2))
     return result
 
 
@@ -358,11 +370,22 @@
 ):
     t, s = lax.axis_index(names[0]), lax.axis_index(names[1])
     barrier = pltpu.get_barrier_semaphore()
-    peers = peers_of(t, s, times, sources)
+    peers, late_peers = peers_of(t, s, False), peers_of(t, s, True)
     count = len(peers)
-
-    def device(k):
-        return {names[0]: peers[k][0], names[1]: peers[k][1]}
+    early = planes // 2
+
+    def device(peer):
+        return {names[0]: peer[0], names[1]: peer[1]}
+
+    def send_to(peer, at):
+        pltpu.make_async_remote_copy(
+            src_ref=send.at[peer[0] * sources + peer[1], at],
+            dst_ref=got.at[t * sources + s, at],
+            send_sem=send_sem,
+            recv_sem=recv_sem,
+            device_id=device(peer),
+            device_id_type=pl.DeviceIdType.MESH,
+        ).start()
 
     def load(p, which):
         source, target = ((one_hbm, one_ref), (two_hbm, two_ref))[which]
@@ -377,8 +400,8 @@
     ]
     for which in (1, 0):
         load(0, which).start()
-    for k in range(count):
-        pl.semaphore_signal(barrier, inc=1, device_id=device(k), device_id_type=pl.DeviceIdType.MESH)
+    for peer in peers:
+        pl.semaphore_signal(barrier, inc=1, device_id=device(peer), device_id_type=pl.DeviceIdType.MESH)
     for copy in table_copies[:3]:
         copy.start()
     for p in range(1, planes):
@@ -407,26 +430,23 @@
         def _():
             pl.semaphore_wait(barrier, count)
 
-        for k in range(count):
-            to_t, to_s = peers[k]
-            pltpu.make_async_remote_copy(
-                src_ref=send.at[to_t * sources + to_s, p],
-                dst_ref=got.at[t * sources + s, p],
-                send_sem=send_sem,
-                recv_sem=recv_sem,
-                device_id=device(k),
-                device_id_type=pl.DeviceIdType.MESH,
-            ).start()
+        @pl.when(p < early)
+        def _():
+            for peer in peers:
+                send_to(peer, p)
+
         own = t * sources + s
         got[own, p, :, :] = send[own, p, :, :]
 
+    for peer in late_peers:
+        send_to(peer, pl.ds(early, planes - early))
     table_copies[3].wait()
     everything = pltpu.make_async_remote_copy(
         src_ref=send.at[pl.ds(0, count)],
         dst_ref=got.at[pl.ds(0, count)],
         send_sem=send_sem,
         recv_sem=recv_sem,
-        device_id=device(0),
+        device_id=device(peers[0]),
         device_id_type=pl.DeviceIdType.MESH,
     )
     everything.wait_recv()

time: 22.2 us -> 19.9 us (0.90)
  the two profiles are of different devices: /device:TPU:0 before, /device:TPU:9 now
where the time goes in v3:
time: 19.9 us; the launch traced here: 19.7 us
  Pallas kernels  19.7 us (99%)
    pallas_call x1, Pallas kernels, fast_device(): pl.pallas_call(functools.partial(exchange_kernel, tables, tiles, planes,...  18.3 us
    pallas_call x1, Pallas kernels, fast_device(): pl.pallas_call(functools.partial(finish_kernel, times, own), out_shape=ja...  1.42 us

profile of v3, /device:TPU:9, one launch (start us, length us, event | category | flops | bytes accessed | tf_op | source)
XLA Modules:
  0.0 19.7 jit_solution(17619747027348190960)
XLA Ops:
  0.0 18.3 %shard_map.64 = (f32[32,4,8,128]{3,2,1,0:T(8,128)S(1)}, bf16[2,256,256]{2,1,0:T(8,128)(2,1)S(1)}) custom-call(bf16[12,12,64,128]{3,2,1,0:T(8,128)(2,1)} %bitcast.15, bf16[12,12,64,128]{3,2,1,0:T(8,128)(2,1)} %bitcast.16, f32[2,16,128]{2,1,0:T(8,128)} %constant.11.clone.phase_hbm, f32[2,8,128]{2,1,0:T(8,128)} %constant.8.clone.twiddle_hbm, ...), custom_call_target="tpu_custom_call" | custom-call | tf_op jit(solution)/shard_map/pallas_call | solution.py:488
  18.3 1.4 %shard_map.65 = f32[4,4,64,128]{3,2,1,0:T(8,128)} custom-call(f32[32,4,8,128]{3,2,1,0:T(8,128)S(1)} %get-tuple-element.7.got, bf16[2,256,256]{2,1,0:T(8,128)(2,1)S(1)} %get-tuple-element.8.line_ref), custom_call_target="tpu_custom_call" | custom-call | tf_op jit(solution)/shard_map/pallas_call | solution.py:516

commit v4 on v2

--- a/solution.py
+++ b/solution.py
@@ -1,4 +1,5 @@
 import functools
+import itertools
 import math
 
 import jax
@@ -247,60 +248,90 @@
     return total + term if sign > 0 else total - term
 
 
-def site_sums(tables, one_ref, two_ref, wide, turned, mixed, row):
-    left_groups, left_signs, right_groups, right_signs, _ = tables
-    rows = wide.shape[2]
-    even = lax.broadcasted_iota(jnp.int32, (8, LANES), 0) % 2 == 0
-    span = pl.ds(row, rows)
+def widen(sources, targets, row):
+    rows = targets[0].shape[2]
 
     @pl.loop(0, 12)
-    def _(a):
+    def _(sink):
         for c in range(12):
-            value = two_ref[a, c, span, :].astype(jnp.float32)
-            wide[a, c, :, :] = value
-            for at in range(0, rows, 8):
-                piece = value[at : at + 8]
-                turned[a, c, at : at + 8, :] = jnp.where(even, pltpu.roll(piece, 7, 0), pltpu.roll(piece, 1, 0))
-
+            for source, target in zip(sources, targets):
+                target[sink, c, :, :] = source[sink, c, pl.ds(row, rows), :].astype(jnp.float32)
+
+
+def site_sums(tables, one, two, partial, mixed):
+    left_groups, left_signs, right_groups, right_signs, phases = tables
+    tiles = one.shape[2] // 2
+    columns = [spin_columns[first] for first in GROUP_PERMS]
+    left_of = [{a: (half, sign) for half in range(2) for a, sign in left_groups[pair][half]} for pair in range(2)]
+    right_of = [{c: (side, sign) for side in range(2) for c, sign in right_groups[turn][side]} for turn in range(2)]
+
+    def read(ref, at, kind, sign):
+        first, second = (ref[at[0], at[1], pl.ds(part, tiles, stride=2), :] if kind in (part, 2) else None for part in range(2))
+        if kind < 2:
+            return second if kind else first
+        return first + second if sign > 0 else first - second
+
+    def blocks(kind):
+        def step(i, sums):
+            sums = list(sums)
+            for j, q_first, c_first in itertools.product(range(3), (0, 2), (0, 2)):
+                ones = {
+                    (q, c): read(one, (q * 3 + i, c * 3 + j), kind, 1)
+                    for q in (q_first, q_first + 1)
+                    for c in (c_first, c_first + 1)
+                }
+                twos = {}
+                for q, c in ones:
+                    for pair in range(2):
+                        for turn in range(2):
+                            at = (columns[pair][q], columns[turn][c])
+                            if at not in twos:
+                                twos[at] = read(two, (at[0] * 3 + i, at[1] * 3 + j), kind, -1)
+                for q, c in ones:
+                    for pair in range(2):
+                        half, left_sign = left_of[pair][columns[pair][q]]
+                        for turn in range(2):
+                            side, right_sign = right_of[turn][c]
+                            k = ((pair * 2 + half) * 2 + turn) * 2 + side
+                            term = ones[q, c] * twos[columns[pair][q], columns[turn][c]]
+                            sums[k] = add_signed(sums[k], term, left_sign * right_sign)
+            return tuple(sums)
+
+        start = tuple(jnp.zeros((tiles, LANES), jnp.float32) for _ in range(16))
+        return lax.fori_loop(0, 3, step, start)
+
+    for kind in range(2):
+        for k, total in enumerate(blocks(kind)):
+            partial[kind, k, :, :] = total
+    both = blocks(2)
     for pair in range(2):
-        left_columns = spin_columns[GROUP_PERMS[pair]]
-        sums = {}
-        for half in range(2):
-            for turn in range(2):
-                right_columns = spin_columns[GROUP_PERMS[turn]]
+        for turn in range(2):
+            quads = ([], [])
+            for half in range(2):
                 for side in range(2):
-                    straight, crossed = None, None
-                    for a, left_sign in left_groups[pair][half]:
-                        for c, right_sign in right_groups[turn][side]:
-                            for i in range(3):
-                                for j in range(3):
-                                    sink, source = left_columns[a] * 3 + i, c * 3 + j
-                                    first = one_ref[sink, source, span, :].astype(jnp.float32)
-                                    at = (a * 3 + i, right_columns[c] * 3 + j)
-                                    sign = left_sign * right_sign
-                                    straight = add_signed(straight, first * wide[at[0], at[1], :, :], sign)
-                                    crossed = add_signed(crossed, first * turned[at[0], at[1], :, :], sign)
-                    sums[half, turn, side] = (straight, crossed)
-        for mu in (2 * pair, 2 * pair + 1):
-            for nu in range(4):
-                for kind in range(2):
-                    total = None
+                    k = ((pair * 2 + half) * 2 + turn) * 2 + side
+                    straight, crossed = partial[0, k, :, :], partial[1, k, :, :]
+                    quads[0].append(straight + crossed)
+                    quads[1].append(both[k] - (straight - crossed))
+            for nu in (2 * turn, 2 * turn + 1):
+                joined = []
+                for quad in quads:
                     for half in range(2):
-                        for side in range(2):
-                            sign = int(left_signs[mu][half] * right_signs[nu][side])
-                            total = add_signed(total, sums[half, nu // 2, side][kind], sign)
-                    start = (4 * mu + nu) * rows
-                    mixed[kind, start : start + rows, :] = total
-
-
-def plane_blocks(phase_ref, twiddle_ref, plane_ref, mixed, tiles, store):
-    blocks = []
-    for t in range(tiles):
-        straight = [mixed[0, pl.ds(2 * t + part, 16, stride=2 * tiles), :] for part in range(2)]
-        crossed = [mixed[1, pl.ds(2 * t + part, 16, stride=2 * tiles), :] for part in range(2)]
-        re, im = straight[0] + straight[1], crossed[1] - crossed[0]
-        c, s = phase_ref[0], phase_ref[1]
-        blocks.append((c * re - s * im, c * im + s * re))
+                        total = add_signed(None, quad[2 * half], int(right_signs[nu][0]))
+                        joined.append(add_signed(total, quad[2 * half + 1], int(right_signs[nu][1])))
+                for mu in (2 * pair, 2 * pair + 1):
+                    field = 4 * mu + nu
+                    phase = phases[field]
+                    for part in range(2):
+                        sign = (phase.real + phase.imag) * (-1 if part and phase.imag else 1)
+                        total = add_signed(None, joined[2 * part], int(left_signs[mu][0] * sign))
+                        total = add_signed(total, joined[2 * part + 1], int(left_signs[mu][1] * sign))
+                        where = 1 - part if phase.imag else part
+                        mixed[where, field * tiles : (field + 1) * tiles, :] = total
+
+
+def plane_blocks(twiddle_ref, plane_ref, mixed, tiles, store):
+    blocks = [tuple(mixed[part, pl.ds(t, 16, stride=tiles), :] for part in range(2)) for t in range(tiles)]
     spectrum = small_fft(blocks)
     turned = []
     for k, (re, im) in enumerate(spectrum):
@@ -335,34 +366,77 @@
             out_ref[at, f, pl.ds(part, 32, stride=2), :] = done[f]
 
 
-def peers_of(t, s, times, sources):
+def peers_of(t, s):
     y, core, z, x = t // 2, t % 2, s // 2, s % 2
-    own_half, other_half = z // 2 * 2, (1 - z // 2) * 2
-    near, far = (z + 1) % 2, z % 2
-    levels = [other_half, other_half + 1, own_half + near, own_half + far]
-    result = []
-    for level in range(4):
-        for plane in range(8):
-            dy, dx, dc = plane // 4, plane // 2 % 2, plane % 2
-            if level == 3 and plane == 0:
-                continue
-            result.append(((y + dy) % 2 * 2 + (core + dc) % 2, levels[level] * 2 + (x + dx) % 2))
-    return result
+    beyond = z // 2
+    edge = 3 * (1 - beyond)
+    inner = edge + 2 * beyond - 1
+    near = beyond * 2 + (z + 1) % 2
+    here = y * 2 + x
+    first, second = here % 2 * (1 - here // 2), (1 - here % 2) * (here // 2)
+    others = ((3 - here) // 3 * 3, 1 + first, 2 + first + second)
+    turn = [(here + k) % 4 for k in range(4)]
+    head = [0] + [1 + (here + k) % 3 for k in range(3)]
+    edges = [beyond * head[k] + (1 - beyond) * turn[k] for k in range(4)]
+    inners = [beyond * head[k] + (1 - beyond) * turn[k] for k in range(4)]
+
+    def chip(level, at):
+        return [(at // 2 * 2 + (core + dc) % 2, level * 2 + at % 2) for dc in (1, 0)]
+
+    across = [
+        ((y + plane // 4) % 2 * 2 + (core + plane) % 2, level * 2 + (x + plane // 2) % 2)
+        for plane in reversed(range(8))
+        for level in (edge, inner)
+    ]
+    late = []
+    late += [(False, peer) for peer in chip(near, head[0])]
+    late += [(False, peer) for peer in chip(z, others[0])]
+    late += [(True, peer) for peer in chip(edge, edges[0])]
+    late += [(False, peer) for peer in chip(near, head[1])]
+    late += [(True, peer) for peer in chip(edge, edges[1])]
+    late += [(False, peer) for peer in chip(z, others[1])]
+    late += [(True, peer) for peer in chip(inner, inners[0])]
+    late += [(False, peer) for peer in chip(near, head[2])]
+    late += [(True, peer) for peer in chip(edge, edges[2])]
+    late += [(False, peer) for peer in chip(z, others[2])]
+    late += [(True, peer) for peer in chip(inner, inners[1])]
+    late += [(False, peer) for peer in chip(near, head[3])]
+    late += [(True, peer) for peer in chip(edge, edges[3])]
+    late += [(True, peer) for peer in chip(inner, inners[2])]
+    late += [(True, peer) for peer in chip(inner, inners[3])]
+    late.append((False, (y * 2 + 1 - core, s)))
+    return across, late, (t, (3 - z) * 2 + x)
 
 
 def exchange_kernel(
     tables, tiles, planes, times, sources, names,
-    one_hbm, two_hbm, phase_hbm, twiddle_hbm, plane_hbm, line_hbm, got, line_out,
-    one_ref, two_ref, phase_ref, twiddle_ref, plane_ref, wide, turned, mixed, send,
-    in_sem, table_sem, send_sem, recv_sem,
+    one_hbm, two_hbm, twiddle_hbm, plane_hbm, line_hbm, got, line_out,
+    one_ref, two_ref, twiddle_ref, plane_ref, one_wide, two_wide, partial, mixed, send,
+    in_sem, table_sem, send_sem, recv_sem, ready,
 ):
     t, s = lax.axis_index(names[0]), lax.axis_index(names[1])
     barrier = pltpu.get_barrier_semaphore()
-    peers = peers_of(t, s, times, sources)
-    count = len(peers)
-
-    def device(k):
-        return {names[0]: peers[k][0], names[1]: peers[k][1]}
+    across, late_peers, mirror = peers_of(t, s)
+    count = times * sources - 1
+    early = planes // 2
+
+    def move(source, target, peer):
+        return pltpu.make_async_remote_copy(
+            src_ref=source,
+            dst_ref=target,
+            send_sem=send_sem,
+            recv_sem=recv_sem,
+            device_id={names[0]: peer[0], names[1]: peer[1]},
+            device_id_type=pl.DeviceIdType.MESH,
+        )
+
+    def send_to(peer, at):
+        move(send.at[peer[0] * sources + peer[1], at], got.at[t * sources + s, at], peer).start()
+
+    def signal(sem, peer):
+        pl.semaphore_signal(
+            sem, inc=1, device_id={names[0]: peer[0], names[1]: peer[1]}, device_id_type=pl.DeviceIdType.MESH
+        )
 
     def load(p, which):
         source, target = ((one_hbm, one_ref), (two_hbm, two_ref))[which]
@@ -372,63 +446,56 @@
     table_copies = [
         pltpu.make_async_copy(source, target, table_sem.at[k])
         for k, (source, target) in enumerate(
-            ((phase_hbm, phase_ref), (twiddle_hbm, twiddle_ref), (plane_hbm, plane_ref), (line_hbm, line_out))
+            ((twiddle_hbm, twiddle_ref), (plane_hbm, plane_ref), (line_hbm, line_out))
         )
     ]
     for which in (1, 0):
         load(0, which).start()
-    for k in range(count):
-        pl.semaphore_signal(barrier, inc=1, device_id=device(k), device_id_type=pl.DeviceIdType.MESH)
-    for copy in table_copies[:3]:
+    for peer in across:
+        signal(barrier, peer)
+    for copy in table_copies[:2]:
         copy.start()
     for p in range(1, planes):
         for which in (1, 0):
             load(p, which).start()
-    table_copies[3].start()
+    table_copies[2].start()
 
     @pl.loop(0, planes)
     def _(p):
         load(p, 1).wait()
         load(p, 0).wait()
         row = pl.multiple_of(p * 2 * tiles, 2 * tiles)
-        site_sums(tables, one_ref, two_ref, wide, turned, mixed, row)
+        widen((two_ref, one_ref), (two_wide, one_wide), row)
+        site_sums(tables, one_wide, two_wide, partial, mixed)
 
         @pl.when(p == 0)
         def _():
-            for copy in table_copies[:3]:
+            for copy in table_copies[:2]:
                 copy.wait()
 
         def store(owner, group, value):
             send[group * sources + owner, p, :, :] = value
 
-        plane_blocks(phase_ref, twiddle_ref, plane_ref, mixed, tiles, store)
+        plane_blocks(twiddle_ref, plane_ref, mixed, tiles, store)
 
         @pl.when(p == 0)
         def _():
-            pl.semaphore_wait(barrier, count)
-
-        for k in range(count):
-            to_t, to_s = peers[k]
-            pltpu.make_async_remote_copy(
-                src_ref=send.at[to_t * sources + to_s, p],
-                dst_ref=got.at[t * sources + s, p],
-                send_sem=send_sem,
-                recv_sem=recv_sem,
-                device_id=device(k),
-                device_id_type=pl.DeviceIdType.MESH,
-            ).start()
+            pl.semaphore_wait(barrier, len(across))
+            signal(ready, mirror)
+
+        @pl.when(p < early)
+        def _():
+            for peer in across:
+                send_to(peer, p)
+
         own = t * sources + s
         got[own, p, :, :] = send[own, p, :, :]
 
-    table_copies[3].wait()
-    everything = pltpu.make_async_remote_copy(
-        src_ref=send.at[pl.ds(0, count)],
-        dst_ref=got.at[pl.ds(0, count)],
-        send_sem=send_sem,
-        recv_sem=recv_sem,
-        device_id=device(0),
-        device_id_type=pl.DeviceIdType.MESH,
-    )
+    pl.semaphore_wait(ready, 1)
+    for crossing, peer in late_peers:
+        send_to(peer, pl.ds(early, planes - early) if crossing else pl.ds(0, planes))
+    table_copies[2].wait()
+    everything = move(send.at[pl.ds(0, count)], got.at[pl.ds(0, count)], mirror)
     everything.wait_recv()
     everything.wait_send()
 
@@ -454,8 +521,6 @@
     tables = spin_tables()
     twiddle, plane_table = plane_tables(L)
     line = line_table(L, own, sources)
-    phase = np.broadcast_to(tables[4][:, None], (16, LANES))
-    phase = jnp.asarray(np.stack([phase.real, phase.imag]), jnp.float32)
 
     def paired(prop):
         split = prop.reshape(2, 12, 12, slab // LANES, LANES).transpose(1, 2, 3, 0, 4)
@@ -464,7 +529,7 @@
     anywhere = pl.BlockSpec(memory_space=pltpu.HBM)
     vmem = pl.BlockSpec(memory_space=pltpu.VMEM)
     everyone = times * sources
-    inputs = (paired(prop_one), paired(prop_two), phase, twiddle, plane_table, line)
+    inputs = (paired(prop_one), paired(prop_two), twiddle, plane_table, line)
     got, line_near = pl.pallas_call(
         functools.partial(exchange_kernel, tables, tiles, planes, times, sources, ("ta", "xyz")),
         out_shape=(
@@ -476,17 +541,18 @@
         scratch_shapes=[
             pltpu.VMEM((12, 12, slab // LANES * 2, LANES), jnp.bfloat16),
             pltpu.VMEM((12, 12, slab // LANES * 2, LANES), jnp.bfloat16),
-            pltpu.VMEM(phase.shape, phase.dtype),
             pltpu.VMEM(twiddle.shape, twiddle.dtype),
             pltpu.VMEM(plane_table.shape, plane_table.dtype),
             pltpu.VMEM((12, 12, 2 * tiles, LANES), jnp.float32),
             pltpu.VMEM((12, 12, 2 * tiles, LANES), jnp.float32),
-            pltpu.VMEM((2, 16 * 2 * tiles, LANES), jnp.float32),
+            pltpu.VMEM((2, 16, tiles, LANES), jnp.float32),
+            pltpu.VMEM((2, 16 * tiles, LANES), jnp.float32),
             pltpu.VMEM((everyone, planes, 8, LANES), jnp.float32),
             pltpu.SemaphoreType.DMA((2, planes)),
-            pltpu.SemaphoreType.DMA((4,)),
+            pltpu.SemaphoreType.DMA((3,)),
             pltpu.SemaphoreType.DMA,
             pltpu.SemaphoreType.DMA,
+            pltpu.SemaphoreType.REGULAR,
         ],
         compiler_params=pltpu.CompilerParams(
             collective_id=0, has_side_effects=True, vmem_limit_bytes=40 * 2**20

time: 22.2 us -> 18.9 us (0.85)
  the two profiles are of different devices: /device:TPU:0 before, /device:TPU:17 now
where the time goes in v4:
time: 18.9 us; the launch traced here: 18.8 us
  Pallas kernels  18.8 us (99%)
    pallas_call x1, Pallas kernels, fast_device(): pl.pallas_call(functools.partial(exchange_kernel, tables, tiles, planes,...  17.4 us
    pallas_call x1, Pallas kernels, fast_device(): pl.pallas_call(functools.partial(finish_kernel, times, own), out_shape=ja...  1.42 us

profile of v4, /device:TPU:17, one launch (start us, length us, event | category | flops | bytes accessed | tf_op | source)
XLA Modules:
  0.0 18.8 jit_solution(13715887540623353710)
XLA Ops:
  0.0 17.4 %shard_map.55 = (f32[32,4,8,128]{3,2,1,0:T(8,128)S(1)}, bf16[2,256,256]{2,1,0:T(8,128)(2,1)S(1)}) custom-call(bf16[12,12,64,128]{3,2,1,0:T(8,128)(2,1)} %bitcast.15, bf16[12,12,64,128]{3,2,1,0:T(8,128)(2,1)} %bitcast.16, f32[2,8,128]{2,1,0:T(8,128)} %constant.6.clone.twiddle_hbm, bf16[2,256,256]{2,1,0:T(8,128)(2,1)} %constant.7.clone.plane_hbm, ...), custom_call_target="tpu_custom_call" | custom-call | tf_op jit(solution)/shard_map/pallas_call | solution.py:533
  17.4 1.4 %shard_map.56 = f32[4,4,64,128]{3,2,1,0:T(8,128)} custom-call(f32[32,4,8,128]{3,2,1,0:T(8,128)S(1)} %get-tuple-element.7.got, bf16[2,256,256]{2,1,0:T(8,128)(2,1)S(1)} %get-tuple-element.8.line_ref), custom_call_target="tpu_custom_call" | custom-call | tf_op jit(solution)/shard_map/pallas_call | solution.py:562

commit v5 on v4

--- a/solution.py
+++ b/solution.py
@@ -131,6 +131,7 @@
 
 LANES = 128
 GROUP_PERMS = (0, 2)
+LATE, AROUND, BULK = range(3)
 
 
 def spin_tables():
@@ -227,18 +228,18 @@
 def swap_blocks(values):
     width = LANES // 4
     shape = values[0].shape
-    block = lax.broadcasted_iota(jnp.int32, shape, len(shape) - 1) // width
     axis = len(shape) - 1
+    block = lax.broadcasted_iota(jnp.int32, shape, axis) // width
+    low, even = block < 2, block % 2 == 0
     values = list(values)
-    for step in (2, 1):
-        keep = (block // step) % 2 == 0
-        result = [None] * 4
-        for i in range(4):
-            if (i // step) % 2 == 0:
-                a, b = values[i], values[i + step]
-                result[i] = jnp.where(keep, a, pltpu.roll(b, step * width, axis))
-                result[i + step] = jnp.where(keep, pltpu.roll(a, LANES - step * width, axis), b)
-        values = result
+    for i in range(2):
+        first, second = values[i], values[i + 2]
+        moved = pltpu.roll(jnp.where(low, second, first), 2 * width, axis)
+        values[i], values[i + 2] = jnp.where(low, first, moved), jnp.where(low, moved, second)
+    for i in (0, 2):
+        first, second = values[i], values[i + 1]
+        values[i] = jnp.where(even, first, pltpu.roll(second, width, axis))
+        values[i + 1] = jnp.where(even, pltpu.roll(first, LANES - width, axis), second)
     return values
 
 
@@ -383,55 +384,53 @@
     def chip(level, at):
         return [(at // 2 * 2 + (core + dc) % 2, level * 2 + at % 2) for dc in (1, 0)]
 
-    across = [
-        ((y + plane // 4) % 2 * 2 + (core + plane) % 2, level * 2 + (x + plane // 2) % 2)
-        for plane in reversed(range(8))
-        for level in (edge, inner)
-    ]
+    beside = chip(z, others[0]) + chip(z, others[1]) + chip(z, others[2]) + [(y * 2 + 1 - core, s)]
     late = []
-    late += [(False, peer) for peer in chip(near, head[0])]
-    late += [(False, peer) for peer in chip(z, others[0])]
-    late += [(True, peer) for peer in chip(edge, edges[0])]
-    late += [(False, peer) for peer in chip(near, head[1])]
-    late += [(True, peer) for peer in chip(edge, edges[1])]
-    late += [(False, peer) for peer in chip(z, others[1])]
-    late += [(True, peer) for peer in chip(inner, inners[0])]
-    late += [(False, peer) for peer in chip(near, head[2])]
-    late += [(True, peer) for peer in chip(edge, edges[2])]
-    late += [(False, peer) for peer in chip(z, others[2])]
-    late += [(True, peer) for peer in chip(inner, inners[1])]
-    late += [(False, peer) for peer in chip(near, head[3])]
-    late += [(True, peer) for peer in chip(edge, edges[3])]
-    late += [(True, peer) for peer in chip(inner, inners[2])]
-    late += [(True, peer) for peer in chip(inner, inners[3])]
-    late.append((False, (y * 2 + 1 - core, s)))
-    return across, late, (t, (3 - z) * 2 + x)
+    late += [peer for peer in chip(z, others[0])]
+    late += [peer for peer in chip(near, head[0])]
+    late += [peer for peer in chip(edge, edges[0])]
+    late += [peer for peer in chip(near, head[1])]
+    late += [peer for peer in chip(z, others[1])]
+    late += [peer for peer in chip(near, head[2])]
+    late += [peer for peer in chip(z, others[2])]
+    late += [peer for peer in chip(near, head[3])]
+    late.append((y * 2 + 1 - core, s))
+    late += [peer for peer in chip(edge, edges[1])]
+    late += [peer for peer in chip(inner, inners[0])]
+    late += [peer for peer in chip(edge, edges[2])]
+    late += [peer for peer in chip(inner, inners[1])]
+    late += [peer for peer in chip(edge, edges[3])]
+    late += [peer for peer in chip(inner, inners[2])]
+    late += [peer for peer in chip(inner, inners[3])]
+    return (edge, inner, near), beside, late
 
 
 def exchange_kernel(
     tables, tiles, planes, times, sources, names,
     one_hbm, two_hbm, twiddle_hbm, plane_hbm, line_hbm, got, line_out,
-    one_ref, two_ref, twiddle_ref, plane_ref, one_wide, two_wide, partial, mixed, send,
-    in_sem, table_sem, send_sem, recv_sem, ready,
+    one_ref, two_ref, twiddle_ref, plane_ref, one_wide, two_wide, partial, mixed, send, relay,
+    in_sem, table_sem, send_sem, recv_sem, relay_sem, ready,
 ):
     t, s = lax.axis_index(names[0]), lax.axis_index(names[1])
     barrier = pltpu.get_barrier_semaphore()
-    across, late_peers, mirror = peers_of(t, s)
-    count = times * sources - 1
-    early = planes // 2
-
-    def move(source, target, peer):
+    z, x = s // 2, s % 2
+    levels, beside, late_peers = peers_of(t, s)
+    (edge, inner, near), count, early = levels, times * sources - 1, planes // 2
+    column = [(t, level * 2 + x) for level in levels]
+    plane_size, late = times * 2, pl.ds(early, planes - early)
+
+    def slot(peer):
+        return peer[1] // 2 * plane_size + peer[0] * 2 + peer[1] % 2
+
+    def move(source, target, peer, kind, landed=None):
         return pltpu.make_async_remote_copy(
             src_ref=source,
             dst_ref=target,
-            send_sem=send_sem,
-            recv_sem=recv_sem,
+            send_sem=send_sem.at[kind],
+            recv_sem=recv_sem.at[kind] if landed is None else landed,
             device_id={names[0]: peer[0], names[1]: peer[1]},
             device_id_type=pl.DeviceIdType.MESH,
         )
-
-    def send_to(peer, at):
-        move(send.at[peer[0] * sources + peer[1], at], got.at[t * sources + s, at], peer).start()
 
     def signal(sem, peer):
         pl.semaphore_signal(
@@ -451,19 +450,25 @@
     ]
     for which in (1, 0):
         load(0, which).start()
-    for peer in across:
+    for peer in column + beside:
         signal(barrier, peer)
     for copy in table_copies[:2]:
         copy.start()
-    for p in range(1, planes):
-        for which in (1, 0):
-            load(p, which).start()
-    table_copies[2].start()
+    for which in (1, 0):
+        load(1, which).start()
 
     @pl.loop(0, planes)
     def _(p):
         load(p, 1).wait()
         load(p, 0).wait()
+
+        @pl.when(p == 0)
+        def _():
+            for later in range(2, planes):
+                for which in (1, 0):
+                    load(later, which).start()
+            table_copies[2].start()
+
         row = pl.multiple_of(p * 2 * tiles, 2 * tiles)
         widen((two_ref, one_ref), (two_wide, one_wide), row)
         site_sums(tables, one_wide, two_wide, partial, mixed)
@@ -474,30 +479,43 @@
                 copy.wait()
 
         def store(owner, group, value):
-            send[group * sources + owner, p, :, :] = value
+            send[slot((group, owner)), p, :, :] = value
 
         plane_blocks(twiddle_ref, plane_ref, mixed, tiles, store)
 
         @pl.when(p == 0)
         def _():
-            pl.semaphore_wait(barrier, len(across))
-            signal(ready, mirror)
+            pl.semaphore_wait(barrier, len(column + beside))
+            for peer in column:
+                signal(ready, peer)
 
         @pl.when(p < early)
         def _():
-            for peer in across:
-                send_to(peer, p)
-
-        own = t * sources + s
-        got[own, p, :, :] = send[own, p, :, :]
-
-    pl.semaphore_wait(ready, 1)
-    for crossing, peer in late_peers:
-        send_to(peer, pl.ds(early, planes - early) if crossing else pl.ds(0, planes))
+            for level, peer in zip(levels, column):
+                group = pl.ds(level * plane_size, plane_size)
+                move(send.at[group, p], relay.at[z, :, p], peer, BULK, relay_sem.at[z]).start()
+
+        got[t * sources + s, p, :, :] = send[slot((t, s)), p, :, :]
+
+    pl.semaphore_wait(ready, len(column))
+    for peer in late_peers:
+        move(send.at[slot(peer), late], got.at[t * sources + s, late], peer, LATE).start()
+    first = pl.ds(0, early)
+    for peer in beside:
+        move(send.at[slot(peer), first], got.at[t * sources + s, first], peer, AROUND).start()
+    for level in (near, edge, inner):
+        move(relay.at[level], relay.at[level], column[0], BULK, relay_sem.at[level]).wait_recv()
+        here = t * sources + level * 2 + x
+        for peer in beside:
+            move(relay.at[level, peer[0] * 2 + peer[1] % 2], got.at[here, first], peer, AROUND).start()
+        got[here, first, :, :] = relay[level, t * 2 + x, :, :, :]
     table_copies[2].wait()
-    everything = move(send.at[pl.ds(0, count)], got.at[pl.ds(0, count)], mirror)
-    everything.wait_recv()
-    everything.wait_send()
+    for kind, number in ((LATE, count), (AROUND, (len(column) + 1) * len(beside)), (BULK, len(column) * plane_size)):
+        span = pl.ds(0, number)
+        total = move(send.at[span, first], got.at[span, first], column[0], kind)
+        if kind != BULK:
+            total.wait_recv()
+        total.wait_send()
 
 
 def finish_kernel(times, own, got, line_ref, out_hbm, out_ref, out_sem):
@@ -548,10 +566,12 @@
             pltpu.VMEM((2, 16, tiles, LANES), jnp.float32),
             pltpu.VMEM((2, 16 * tiles, LANES), jnp.float32),
             pltpu.VMEM((everyone, planes, 8, LANES), jnp.float32),
+            pltpu.VMEM((sources // 2, times * 2, planes // 2, 8, LANES), jnp.float32),
             pltpu.SemaphoreType.DMA((2, planes)),
             pltpu.SemaphoreType.DMA((3,)),
-            pltpu.SemaphoreType.DMA,
-            pltpu.SemaphoreType.DMA,
+            pltpu.SemaphoreType.DMA((3,)),
+            pltpu.SemaphoreType.DMA((2,)),
+            pltpu.SemaphoreType.DMA((sources // 2,)),
             pltpu.SemaphoreType.REGULAR,
         ],
         compiler_params=pltpu.CompilerParams(

time: 18.9 us -> 18.8 us (level)
  the two profiles are of different devices: /device:TPU:17 before, /device:TPU:0 now
where the time goes in v5:
time: 18.8 us; the launch traced here: 18.6 us
  Pallas kernels  18.6 us (99%)
    pallas_call x1, Pallas kernels, fast_device(): pl.pallas_call(functools.partial(exchange_kernel, tables, tiles, planes,...  17.2 us
    pallas_call x1, Pallas kernels, fast_device(): pl.pallas_call(functools.partial(finish_kernel, times, own), out_shape=ja...  1.4 us

profile of v5, /device:TPU:0, one launch (start us, length us, event | category | flops | bytes accessed | tf_op | source)
XLA Modules:
  0.0 18.6 jit_solution(9792292152777065042)
XLA Ops:
  0.0 17.2 %shard_map.55 = (f32[32,4,8,128]{3,2,1,0:T(8,128)S(1)}, bf16[2,256,256]{2,1,0:T(8,128)(2,1)S(1)}) custom-call(bf16[12,12,64,128]{3,2,1,0:T(8,128)(2,1)} %bitcast.15, bf16[12,12,64,128]{3,2,1,0:T(8,128)(2,1)} %bitcast.16, f32[2,8,128]{2,1,0:T(8,128)} %constant.6.clone.twiddle_hbm, bf16[2,256,256]{2,1,0:T(8,128)(2,1)} %constant.7.clone.plane_hbm, ...), custom_call_target="tpu_custom_call" | custom-call | tf_op jit(solution)/shard_map/pallas_call | solution.py:551
  17.2 1.4 %shard_map.56 = f32[4,4,64,128]{3,2,1,0:T(8,128)} custom-call(f32[32,4,8,128]{3,2,1,0:T(8,128)S(1)} %get-tuple-element.7.got, bf16[2,256,256]{2,1,0:T(8,128)(2,1)S(1)} %get-tuple-element.8.line_ref), custom_call_target="tpu_custom_call" | custom-call | tf_op jit(solution)/shard_map/pallas_call | solution.py:582

commit v6 on v5

--- a/solution.py
+++ b/solution.py
@@ -416,6 +416,7 @@
     z, x = s // 2, s % 2
     levels, beside, late_peers = peers_of(t, s)
     (edge, inner, near), count, early = levels, times * sources - 1, planes // 2
+    levels = (near, edge, inner)
     column = [(t, level * 2 + x) for level in levels]
     plane_size, late = times * 2, pl.ds(early, planes - early)
 

time: 18.8 us -> 18.7 us (level)
  no operation moved by 1% of the time
where the time goes in v6:
time: 18.7 us; the launch traced here: 18.6 us
  Pallas kernels  18.6 us (99%)
    pallas_call x1, Pallas kernels, fast_device(): pl.pallas_call(functools.partial(exchange_kernel, tables, tiles, planes,...  17.2 us
    pallas_call x1, Pallas kernels, fast_device(): pl.pallas_call(functools.partial(finish_kernel, times, own), out_shape=ja...  1.4 us

profile of v6, /device:TPU:0, one launch (start us, length us, event | category | flops | bytes accessed | tf_op | source)
XLA Modules:
  0.0 18.6 jit_solution(2097350951819889810)
XLA Ops:
  0.0 17.2 %shard_map.55 = (f32[32,4,8,128]{3,2,1,0:T(8,128)S(1)}, bf16[2,256,256]{2,1,0:T(8,128)(2,1)S(1)}) custom-call(bf16[12,12,64,128]{3,2,1,0:T(8,128)(2,1)} %bitcast.15, bf16[12,12,64,128]{3,2,1,0:T(8,128)(2,1)} %bitcast.16, f32[2,8,128]{2,1,0:T(8,128)} %constant.6.clone.twiddle_hbm, bf16[2,256,256]{2,1,0:T(8,128)(2,1)} %constant.7.clone.plane_hbm, ...), custom_call_target="tpu_custom_call" | custom-call | tf_op jit(solution)/shard_map/pallas_call | solution.py:552
  17.2 1.4 %shard_map.56 = f32[4,4,64,128]{3,2,1,0:T(8,128)} custom-call(f32[32,4,8,128]{3,2,1,0:T(8,128)S(1)} %get-tuple-element.7.got, bf16[2,256,256]{2,1,0:T(8,128)(2,1)S(1)} %get-tuple-element.8.line_ref), custom_call_target="tpu_custom_call" | custom-call | tf_op jit(solution)/shard_map/pallas_call | solution.py:583

commit v7 on v5

--- a/solution.py
+++ b/solution.py
@@ -132,6 +132,7 @@
 LANES = 128
 GROUP_PERMS = (0, 2)
 LATE, AROUND, BULK = range(3)
+TOGETHER = 2
 
 
 def spin_tables():
@@ -192,7 +193,9 @@
     parts = complex_block(turn).reshape(2, sources, length // sources, 2, length)
     full = np.einsum("asxbk,fg->sxafbgk", parts, np.eye(own))
     rows = length * 2 * own
-    return high_low(full.reshape(rows, rows))
+    full = full.reshape(rows, 2, rows // 2)
+    moved = np.roll(full, length, axis=2)
+    return jnp.concatenate([high_low(full.reshape(rows, rows)), high_low(moved.reshape(rows, rows))])
 
 
 def split_dot(values, table):
@@ -358,51 +361,79 @@
                 store(owner, 2 * pair + 1, jnp.where(upper, pltpu.roll(re, 4, 0), im))
 
 
-def finish_time(rows, line_ref, out_ref, at, own):
-    out = split_dot(rows.T, line_ref)
-    for part in range(2):
-        grid = out[:, part * LANES : (part + 1) * LANES].reshape(4, 4, 8, LANES)
-        done = swap_blocks([grid[:, q].reshape(32, LANES) for q in range(4)])
-        for f in range(own):
-            out_ref[at, f, pl.ds(part, 32, stride=2), :] = done[f]
-
-
-def peers_of(t, s):
+def finish_times(blocks, line_ref, out_ref, first, own):
+    operands = ([], [])
+    for rows in blocks:
+        grid = rows.T.reshape(4, 4, 8, -1)
+        for q in range(4):
+            operands[q % 2].append(grid[:, q].reshape(32, -1))
+    out = [split_dot(jnp.concatenate(operands[k], axis=0), (line_ref[2 * k], line_ref[2 * k + 1])) for k in range(2)]
+    block = lax.broadcasted_iota(jnp.int32, (32, LANES), 1) // L
+    low, even = block < 2, block % 2 == 0
+    for at in range(len(blocks)):
+        for part in range(2):
+            lanes = slice(part * LANES, (part + 1) * LANES)
+            pairs = []
+            for half in range(2):
+                start = (2 * at + half) * 32
+                plain, moved = (out[k][start : start + 32, lanes] for k in range(2))
+                crossed = pltpu.roll(jnp.where(even, moved, plain), LANES - L, 1)
+                pairs.append((jnp.where(even, plain, moved), crossed))
+            for f in range(2):
+                left, right = pairs[0][f], pairs[1][f]
+                swapped = pltpu.roll(jnp.where(low, right, left), LANES // 2, 1)
+                out_ref[first + at, f, pl.ds(part, 32, stride=2), :] = jnp.where(low, left, swapped)
+                out_ref[first + at, f + 2, pl.ds(part, 32, stride=2), :] = jnp.where(low, swapped, right)
+
+
+def levels_of(s):
+    z = s // 2
+    beyond = z // 2
+    edge = 3 * (1 - beyond)
+    return edge, edge + 2 * beyond - 1, beyond * 2 + (z + 1) % 2
+
+
+def chip(core, level, at):
+    return [(at // 2 * 2 + (core + dc) % 2, level * 2 + at % 2) for dc in (1, 0)]
+
+
+def others_of(t, s):
+    here = t // 2 * 2 + s % 2
+    first, second = here % 2 * (1 - here // 2), (1 - here % 2) * (here // 2)
+    return (3 - here) // 3 * 3, 1 + first, 2 + first + second
+
+
+def beside_of(t, s):
+    return [peer for at in others_of(t, s) for peer in chip(t % 2, s // 2, at)] + [(t // 2 * 2 + 1 - t % 2, s)]
+
+
+def late_of(t, s):
     y, core, z, x = t // 2, t % 2, s // 2, s % 2
     beyond = z // 2
-    edge = 3 * (1 - beyond)
-    inner = edge + 2 * beyond - 1
-    near = beyond * 2 + (z + 1) % 2
+    edge, inner, near = levels_of(s)
     here = y * 2 + x
-    first, second = here % 2 * (1 - here // 2), (1 - here % 2) * (here // 2)
-    others = ((3 - here) // 3 * 3, 1 + first, 2 + first + second)
+    others = others_of(t, s)
     turn = [(here + k) % 4 for k in range(4)]
     head = [0] + [1 + (here + k) % 3 for k in range(3)]
-    edges = [beyond * head[k] + (1 - beyond) * turn[k] for k in range(4)]
-    inners = [beyond * head[k] + (1 - beyond) * turn[k] for k in range(4)]
-
-    def chip(level, at):
-        return [(at // 2 * 2 + (core + dc) % 2, level * 2 + at % 2) for dc in (1, 0)]
-
-    beside = chip(z, others[0]) + chip(z, others[1]) + chip(z, others[2]) + [(y * 2 + 1 - core, s)]
+    edges = inners = [beyond * head[k] + (1 - beyond) * turn[k] for k in range(4)]
     late = []
-    late += [peer for peer in chip(z, others[0])]
-    late += [peer for peer in chip(near, head[0])]
-    late += [peer for peer in chip(edge, edges[0])]
-    late += [peer for peer in chip(near, head[1])]
-    late += [peer for peer in chip(z, others[1])]
-    late += [peer for peer in chip(near, head[2])]
-    late += [peer for peer in chip(z, others[2])]
-    late += [peer for peer in chip(near, head[3])]
+    late += [peer for peer in chip(core, z, others[0])]
+    late += [peer for peer in chip(core, near, head[0])]
+    late += [peer for peer in chip(core, edge, edges[0])]
+    late += [peer for peer in chip(core, near, head[1])]
+    late += [peer for peer in chip(core, z, others[1])]
+    late += [peer for peer in chip(core, near, head[2])]
+    late += [peer for peer in chip(core, z, others[2])]
+    late += [peer for peer in chip(core, near, head[3])]
     late.append((y * 2 + 1 - core, s))
-    late += [peer for peer in chip(edge, edges[1])]
-    late += [peer for peer in chip(inner, inners[0])]
-    late += [peer for peer in chip(edge, edges[2])]
-    late += [peer for peer in chip(inner, inners[1])]
-    late += [peer for peer in chip(edge, edges[3])]
-    late += [peer for peer in chip(inner, inners[2])]
-    late += [peer for peer in chip(inner, inners[3])]
-    return (edge, inner, near), beside, late
+    late += [peer for peer in chip(core, edge, edges[1])]
+    late += [peer for peer in chip(core, inner, inners[0])]
+    late += [peer for peer in chip(core, edge, edges[2])]
+    late += [peer for peer in chip(core, inner, inners[1])]
+    late += [peer for peer in chip(core, edge, edges[3])]
+    late += [peer for peer in chip(core, inner, inners[2])]
+    late += [peer for peer in chip(core, inner, inners[3])]
+    return late
 
 
 def exchange_kernel(
@@ -411,12 +442,23 @@
     one_ref, two_ref, twiddle_ref, plane_ref, one_wide, two_wide, partial, mixed, send, relay,
     in_sem, table_sem, send_sem, recv_sem, relay_sem, ready,
 ):
+    def load(p, which):
+        source, target = ((one_hbm, one_ref), (two_hbm, two_ref))[which]
+        rows = pl.ds(pl.multiple_of(p * 2 * tiles, 2 * tiles), 2 * tiles)
+        return pltpu.make_async_copy(source.at[:, :, rows, :], target.at[:, :, rows, :], in_sem.at[which, p])
+
+    @pl.loop(0, 2)
+    def _(p):
+        for which in (1, 0):
+            load(p, which).start()
+
     t, s = lax.axis_index(names[0]), lax.axis_index(names[1])
     barrier = pltpu.get_barrier_semaphore()
     z, x = s // 2, s % 2
-    levels, beside, late_peers = peers_of(t, s)
-    (edge, inner, near), count, early = levels, times * sources - 1, planes // 2
+    edge, inner, near = levels_of(s)
+    levels, count, early = (near, edge, inner), times * sources - 1, planes // 2
     column = [(t, level * 2 + x) for level in levels]
+    beside = beside_of(t, s)
     plane_size, late = times * 2, pl.ds(early, planes - early)
 
     def slot(peer):
@@ -437,25 +479,19 @@
             sem, inc=1, device_id={names[0]: peer[0], names[1]: peer[1]}, device_id_type=pl.DeviceIdType.MESH
         )
 
-    def load(p, which):
-        source, target = ((one_hbm, one_ref), (two_hbm, two_ref))[which]
-        rows = pl.ds(pl.multiple_of(p * 2 * tiles, 2 * tiles), 2 * tiles)
-        return pltpu.make_async_copy(source.at[:, :, rows, :], target.at[:, :, rows, :], in_sem.at[which, p])
-
     table_copies = [
         pltpu.make_async_copy(source, target, table_sem.at[k])
         for k, (source, target) in enumerate(
             ((twiddle_hbm, twiddle_ref), (plane_hbm, plane_ref), (line_hbm, line_out))
         )
     ]
-    for which in (1, 0):
-        load(0, which).start()
     for peer in column + beside:
         signal(barrier, peer)
     for copy in table_copies[:2]:
         copy.start()
-    for which in (1, 0):
-        load(1, which).start()
+    late_peers = [(peer, slot(peer)) for peer in late_of(t, s)]
+    beside_slots = [(peer, slot(peer)) for peer in beside]
+    mine = t * sources + s
 
     @pl.loop(0, planes)
     def _(p):
@@ -498,11 +534,11 @@
         got[t * sources + s, p, :, :] = send[slot((t, s)), p, :, :]
 
     pl.semaphore_wait(ready, len(column))
-    for peer in late_peers:
-        move(send.at[slot(peer), late], got.at[t * sources + s, late], peer, LATE).start()
+    for peer, at in late_peers:
+        move(send.at[at, late], got.at[mine, late], peer, LATE).start()
     first = pl.ds(0, early)
-    for peer in beside:
-        move(send.at[slot(peer), first], got.at[t * sources + s, first], peer, AROUND).start()
+    for peer, at in beside_slots:
+        move(send.at[at, first], got.at[mine, first], peer, AROUND).start()
     for level in (near, edge, inner):
         move(relay.at[level], relay.at[level], column[0], BULK, relay_sem.at[level]).wait_recv()
         here = t * sources + level * 2 + x
@@ -520,13 +556,14 @@
 
 def finish_kernel(times, own, got, line_ref, out_hbm, out_ref, out_sem):
     copies = []
-    for at in range(times):
-        span = got.shape[0] // times
-        rows = got[at * span : (at + 1) * span].reshape(-1, LANES)
-        finish_time(rows, line_ref, out_ref, at, own)
-        copy = pltpu.make_async_copy(out_ref.at[at], out_hbm.at[at], out_sem.at[at])
-        copy.start()
-        copies.append(copy)
+    span = got.shape[0] // times
+    for first in range(0, times, TOGETHER):
+        blocks = [got[at * span : (at + 1) * span].reshape(-1, LANES) for at in range(first, first + TOGETHER)]
+        finish_times(blocks, line_ref, out_ref, first, own)
+        for at in range(first, first + TOGETHER):
+            copy = pltpu.make_async_copy(out_ref.at[at], out_hbm.at[at], out_sem.at[at])
+            copy.start()
+            copies.append(copy)
     for copy in copies:
         copy.wait()
 

time: 18.8 us -> 18.7 us (level)
  no operation moved by 1% of the time
where the time goes in v7:
time: 18.7 us; the launch traced here: 18.5 us
  Pallas kernels  18.5 us (99%)
    pallas_call x1, Pallas kernels, fast_device(): pl.pallas_call(functools.partial(exchange_kernel, tables, tiles, planes,...  17.2 us
    pallas_call x1, Pallas kernels, fast_device(): pl.pallas_call(functools.partial(finish_kernel, times, own), out_shape=ja...  1.36 us

profile of v7, /device:TPU:0, one launch (start us, length us, event | category | flops | bytes accessed | tf_op | source)
XLA Modules:
  0.0 18.5 jit_solution(11143980177078735164)
XLA Ops:
  0.0 17.2 %shard_map.64 = (f32[32,4,8,128]{3,2,1,0:T(8,128)S(1)}, bf16[4,256,256]{2,1,0:T(8,128)(2,1)S(1)}) custom-call(bf16[12,12,64,128]{3,2,1,0:T(8,128)(2,1)} %bitcast.15, bf16[12,12,64,128]{3,2,1,0:T(8,128)(2,1)} %bitcast.16, f32[2,8,128]{2,1,0:T(8,128)} %constant.8.clone.twiddle_hbm, bf16[2,256,256]{2,1,0:T(8,128)(2,1)} %constant.9.clone.plane_hbm, ...), custom_call_target="tpu_custom_call" | custom-call | tf_op jit(solution)/shard_map/pallas_call | solution.py:588
  17.2 1.4 %shard_map.65 = f32[4,4,64,128]{3,2,1,0:T(8,128)} custom-call(f32[32,4,8,128]{3,2,1,0:T(8,128)S(1)} %get-tuple-element.7.got, bf16[4,256,256]{2,1,0:T(8,128)(2,1)S(1)} %get-tuple-element.8.line_ref), custom_call_target="tpu_custom_call" | custom-call | tf_op jit(solution)/shard_map/pallas_call | solution.py:619

commit v8 on v7

--- a/solution.py
+++ b/solution.py
@@ -534,11 +534,11 @@
         got[t * sources + s, p, :, :] = send[slot((t, s)), p, :, :]
 
     pl.semaphore_wait(ready, len(column))
-    for peer, at in late_peers:
-        move(send.at[at, late], got.at[mine, late], peer, LATE).start()
     first = pl.ds(0, early)
     for peer, at in beside_slots:
         move(send.at[at, first], got.at[mine, first], peer, AROUND).start()
+    for peer, at in late_peers:
+        move(send.at[at, late], got.at[mine, late], peer, LATE).start()
     for level in (near, edge, inner):
         move(relay.at[level], relay.at[level], column[0], BULK, relay_sem.at[level]).wait_recv()
         here = t * sources + level * 2 + x

time: 18.7 us -> 18.7 us (level)
  no operation moved by 1% of the time
where the time goes in v8:
time: 18.7 us; the launch traced here: 18.5 us
  Pallas kernels  18.5 us (99%)
    pallas_call x1, Pallas kernels, fast_device(): pl.pallas_call(functools.partial(exchange_kernel, tables, tiles, planes,...  17.1 us
    pallas_call x1, Pallas kernels, fast_device(): pl.pallas_call(functools.partial(finish_kernel, times, own), out_shape=ja...  1.35 us

profile of v8, /device:TPU:0, one launch (start us, length us, event | category | flops | bytes accessed | tf_op | source)
XLA Modules:
  0.0 18.5 jit_solution(5200662278379174349)
XLA Ops:
  0.0 17.1 %shard_map.64 = (f32[32,4,8,128]{3,2,1,0:T(8,128)S(1)}, bf16[4,256,256]{2,1,0:T(8,128)(2,1)S(1)}) custom-call(bf16[12,12,64,128]{3,2,1,0:T(8,128)(2,1)} %bitcast.15, bf16[12,12,64,128]{3,2,1,0:T(8,128)(2,1)} %bitcast.16, f32[2,8,128]{2,1,0:T(8,128)} %constant.8.clone.twiddle_hbm, bf16[2,256,256]{2,1,0:T(8,128)(2,1)} %constant.9.clone.plane_hbm, ...), custom_call_target="tpu_custom_call" | custom-call | tf_op jit(solution)/shard_map/pallas_call | solution.py:588
  17.1 1.4 %shard_map.65 = f32[4,4,64,128]{3,2,1,0:T(8,128)} custom-call(f32[32,4,8,128]{3,2,1,0:T(8,128)S(1)} %get-tuple-element.7.got, bf16[4,256,256]{2,1,0:T(8,128)(2,1)S(1)} %get-tuple-element.8.line_ref), custom_call_target="tpu_custom_call" | custom-call | tf_op jit(solution)/shard_map/pallas_call | solution.py:619

commit v9 on v8

--- a/solution.py
+++ b/solution.py
@@ -456,7 +456,10 @@
     barrier = pltpu.get_barrier_semaphore()
     z, x = s // 2, s % 2
     edge, inner, near = levels_of(s)
-    levels, count, early = (near, edge, inner), times * sources - 1, planes // 2
+    beyond = z // 2
+    second = beyond * edge + (1 - beyond) * inner
+    third = beyond * inner + (1 - beyond) * edge
+    levels, count, early = (near, second, third), times * sources - 1, planes // 2
     column = [(t, level * 2 + x) for level in levels]
     beside = beside_of(t, s)
     plane_size, late = times * 2, pl.ds(early, planes - early)

time: 18.7 us -> 18.7 us (level)
  no operation moved by 1% of the time
where the time goes in v9:
time: 18.7 us; the launch traced here: 18.5 us
  Pallas kernels  18.5 us (99%)
    pallas_call x1, Pallas kernels, fast_device(): pl.pallas_call(functools.partial(exchange_kernel, tables, tiles, planes,...  17.1 us
    pallas_call x1, Pallas kernels, fast_device(): pl.pallas_call(functools.partial(finish_kernel, times, own), out_shape=ja...  1.35 us

profile of v9, /device:TPU:0, one launch (start us, length us, event | category | flops | bytes accessed | tf_op | source)
XLA Modules:
  0.0 18.5 jit_solution(4649603760315141422)
XLA Ops:
  0.0 17.1 %shard_map.64 = (f32[32,4,8,128]{3,2,1,0:T(8,128)S(1)}, bf16[4,256,256]{2,1,0:T(8,128)(2,1)S(1)}) custom-call(bf16[12,12,64,128]{3,2,1,0:T(8,128)(2,1)} %bitcast.15, bf16[12,12,64,128]{3,2,1,0:T(8,128)(2,1)} %bitcast.16, f32[2,8,128]{2,1,0:T(8,128)} %constant.8.clone.twiddle_hbm, bf16[2,256,256]{2,1,0:T(8,128)(2,1)} %constant.9.clone.plane_hbm, ...), custom_call_target="tpu_custom_call" | custom-call | tf_op jit(solution)/shard_map/pallas_call | solution.py:591
  17.1 1.4 %shard_map.65 = f32[4,4,64,128]{3,2,1,0:T(8,128)} custom-call(f32[32,4,8,128]{3,2,1,0:T(8,128)S(1)} %get-tuple-element.7.got, bf16[4,256,256]{2,1,0:T(8,128)(2,1)S(1)} %get-tuple-element.8.line_ref), custom_call_target="tpu_custom_call" | custom-call | tf_op jit(solution)/shard_map/pallas_call | solution.py:622
